TPU v7x, 128 devices: a whole 4x4x4 slice. The times are simulated.
128 devices in a mesh: wide: 16 (over z, x_hi, core), narrow: 8 (over y, x_lo).
Axes of the slice: x: 4 (x_hi: 2, x_lo: 2; x = x_hi * 2 + x_lo), y: 4, z: 4, core: 2. Of those that a mesh axis runs over, the one named last changes fastest.
Arguments:
- homolog_embedding: float32 [64, 1024, 256], P('wide', 'narrow'), may hold values from -6 to 6
- pair_state: float32 [1024, 1024, 128], P('wide', 'narrow'), may hold values from -6 to 6
- probe_projector: float32 [256, 256], replicated, may hold values from -0.375 to 0.375
- lookup_projector: float32 [256, 256], replicated, may hold values from -0.375 to 0.375
- content_projector: float32 [256, 256], replicated, may hold values from -0.375 to 0.375
- sigmoid_projector: float32 [256, 256], replicated, may hold values from -0.375 to 0.375
- sigmoid_offset: float32 [256], replicated, may hold values from -4 to 4
- pair_bias_weight: float32 [128, 8], replicated, may hold values from -4 to 4
- mixing_projector: float32 [256, 256], replicated, may hold values from -0.375 to 0.375
- mixing_offset: float32 [256], replicated, may hold values from -3 to 3
- first_factor_projector: float32 [256, 32], replicated, may hold values from -0.375 to 0.375
- second_factor_projector: float32 [256, 32], replicated, may hold values from -0.375 to 0.375
- outer_product_weight: float32 [1024, 128], replicated, may hold values from -0.5 to 0.5
- outer_product_bias: float32 [128], replicated, may hold values from -3 to 3
- up_weight: float32 [128, 512], replicated, may hold values from -0.5 to 0.5
- expand_bias: float32 [512], replicated, may hold values from -3 to 3
- down_weight: float32 [512, 128], replicated, may hold values from -0.25 to 0.25
Outputs:
- alignment_state_next: float32 [64, 1024, 256], P('wide', 'narrow')
- pair_state_next: float32 [1024, 1024, 128], P('wide', 'narrow')
All inputs are finite; a program needn't handle non-finite values.
Results may differ from a plain program's by a relative error of at most 0.0003.
Values sent between devices are 32-bit elements; how exact they have to be, the bound alone decides.
A program may use at most 128 MiB of HBM per device.

v0:
```python
import math

import jax
import jax.numpy as jnp
from jax import lax
from jax.sharding import PartitionSpec as P

finest_precision = lax.Precision.HIGHEST


def laid_out(blocks, dim):
    blocks = jnp.moveaxis(blocks, 0, dim)
    dims = blocks.shape
    return blocks.reshape(*dims[:dim], dims[dim] * dims[dim + 1], *dims[dim + 2 :])


def copy_for_each(x, axis):
    devices = lax.axis_size(axis)
    return lax.all_to_all(jnp.broadcast_to(x[None], (devices, *x.shape)), axis, 0, 0, tiled=True)


def collect(x, axis, dim):
    return laid_out(copy_for_each(x, axis), dim)


def layer_normalize(tensor):
    row_mean = jnp.mean(tensor, axis=-1, keepdims=True)
    centered = tensor - row_mean
    variance = jnp.mean(centered * centered, axis=-1, keepdims=True)
    return centered * lax.rsqrt(variance + 1e-05)


def matrix_multiply(first_arr, second_arr):
    return jnp.dot(
        first_arr, second_arr, precision=finest_precision, preferred_element_type=jnp.float32
    )


def per_device(
    homolog_embedding,
    pair_state,
    probe_projector,
    lookup_projector,
    content_projector,
    sigmoid_projector,
    sigmoid_offset,
    pair_bias_weight,
    mixing_projector,
    mixing_offset,
    first_factor_projector,
    second_factor_projector,
    outer_product_weight,
    outer_product_bias,
    up_weight,
    expand_bias,
    down_weight,
):
    head_count = pair_bias_weight.shape[1]
    channel_count = homolog_embedding.shape[2]
    head_width = channel_count // head_count
    alignment_normed = layer_normalize(homolog_embedding)
    query_vectors = matrix_multiply(alignment_normed, probe_projector) / math.sqrt(head_width)
    key_rows = matrix_multiply(alignment_normed, lookup_projector)
    value_rows = matrix_multiply(alignment_normed, content_projector)
    gate_logits = matrix_multiply(alignment_normed, sigmoid_projector) + sigmoid_offset
    bias_tile = jnp.einsum(
        "ijc,ch->hij", layer_normalize(pair_state), pair_bias_weight, precision=finest_precision
    )
    own_heads = lax.all_to_all(bias_tile, "narrow", split_axis=0, concat_axis=2, tiled=True)
    pair_bias = lax.all_gather(own_heads, "wide", axis=1, tiled=True)
    operands = (
        lax.all_to_all(query_vectors, "narrow", split_axis=2, concat_axis=1, tiled=True),
        lax.all_to_all(key_rows, "narrow", split_axis=2, concat_axis=1, tiled=True),
        lax.all_to_all(value_rows, "narrow", split_axis=2, concat_axis=1, tiled=True),
        lax.all_to_all(gate_logits, "narrow", split_axis=2, concat_axis=1, tiled=True),
    )
    seq_len = operands[0].shape[1]
    local_width = operands[0].shape[2]
    local_heads = pair_bias.shape[0]
    local_size = local_width // local_heads
    row_span = min(512, seq_len)
    span_count = seq_len // row_span

    def per_item(item_parts):
        query_item = item_parts[0].reshape(seq_len, local_heads, local_size)
        key_item = item_parts[1].reshape(seq_len, local_heads, local_size)
        value_item = item_parts[2].reshape(seq_len, local_heads, local_size)

        def per_block(block_index):
            query_rows = lax.dynamic_slice_in_dim(query_item, block_index * row_span, row_span, 0)
            bias_rows = lax.dynamic_slice_in_dim(pair_bias, block_index * row_span, row_span, 1)
            scores = (
                jnp.einsum("qhd,khd->hqk", query_rows, key_item, precision=finest_precision)
                + bias_rows
            )
            row_max = jnp.max(scores, axis=-1, keepdims=True)
            exponent = jnp.exp(scores - row_max)
            softmax_probabilities = exponent / jnp.sum(exponent, axis=-1, keepdims=True)
            returned_tensor = jnp.einsum(
                "hqk,khd->qhd", softmax_probabilities, value_item, precision=finest_precision
            )
            return returned_tensor.reshape(row_span, local_width)

        blocks = lax.map(per_block, jnp.arange(span_count, dtype=jnp.int32))
        return blocks.reshape(seq_len, local_width)

    outcome = lax.map(per_item, (operands[0], operands[1], operands[2]))
    outcome = outcome * jax.nn.sigmoid(operands[3])
    merged_heads = lax.all_to_all(outcome, "narrow", split_axis=1, concat_axis=2, tiled=True)
    alignment_state_next = (
        homolog_embedding + matrix_multiply(merged_heads, mixing_projector) + mixing_offset
    )
    outer_product_normed = layer_normalize(alignment_state_next)
    left_proj = jnp.einsum(
        "srm,mc->scr", outer_product_normed, first_factor_projector, precision=finest_precision
    )
    right_proj = jnp.einsum(
        "srm,mc->scr", outer_product_normed, second_factor_projector, precision=finest_precision
    )
    left_rows = collect(left_proj, "narrow", 2)
    left_all = lax.all_to_all(left_rows, "wide", split_axis=2, concat_axis=0, tiled=True)
    seq_count = left_all.shape[0]
    tile_rows = left_all.shape[2]
    tile_cols = right_proj.shape[2]
    outer_width = left_all.shape[1] * right_proj.shape[1]
    right_all = collect(right_proj, "wide", 0)
    block_rows = math.gcd(16, tile_rows)

    def outer_block(block_index):
        left_part = lax.dynamic_slice_in_dim(left_all, block_index * block_rows, block_rows, 2)
        product = (
            jnp.einsum("sci,sdj->ijcd", left_part, right_all, precision=finest_precision)
            / seq_count
        )
        flat = product.reshape(block_rows * tile_cols, outer_width)
        return matrix_multiply(flat, outer_product_weight).reshape(block_rows, tile_cols, -1)

    update = lax.map(outer_block, jnp.arange(tile_rows // block_rows, dtype=jnp.int32))
    update = update.reshape(tile_rows, tile_cols, -1)
    pair_mid = pair_state + update + outer_product_bias
    hidden = jax.nn.relu(matrix_multiply(layer_normalize(pair_mid), up_weight) + expand_bias)
    pair_state_next = pair_mid + matrix_multiply(hidden, down_weight)
    return (alignment_state_next, pair_state_next)


def solution(mesh):
    placed = (
        P("wide", "narrow", None),
        P("wide", "narrow", None),
        P(),
        P(),
        P(),
        P(),
        P(),
        P(),
        P(),
        P(),
        P(),
        P(),
        P(),
        P(),
        P(),
        P(),
        P(),
    )
    return jax.shard_map(
        per_device,
        mesh=mesh,
        in_specs=placed,
        out_specs=(P("wide", "narrow", None), P("wide", "narrow", None)),
        check_vma=False,
    )
```

profile of v0, /device:TPU:1, one launch (start us, length us, event | category | flops | bytes accessed | tf_op | source)
XLA Modules:
  0.0 399.1 jit_solution(15442561470067238716)
XLA Ops:
  7.2 3.3 reduce_sum.83
  10.6 4.2 %multiply_reduce_fusion.1 = f32[64,128]{1,0:T(8,128)S(1)} fusion(f32[64,128,128]{2,1,0:T(8,128)} %param.24, f32[64,128]{1,0:T(8,128)S(1)} %broadcast_multiply_fusion.2), kind=kLoop, calls=%fused_computation.37 | loop fusion | flops 3137536 | bytes 4259840 | tf_op jit(solution)/shard_map/reduce_sum | solution.py:29
  14.8 6.4 %fusion.45 = f32[8,64,128]{2,0,1:T(8,128)S(1)} fusion(f32[64,128,128]{2,1,0:T(8,128)S(1)} %copy-done.1, f32[64,128]{1,0:T(8,128)S(1)} %add_rsqrt_fusion.1, f32[64,128]{1,0:T(8,128)S(1)} %broadcast_multiply_fusion.2, f32[128,8]{0,1:T(8,128)S(1)} %copy-done.14), kind=kOutput, calls=%fused_computation.49 | convolution fusion | flops 102760448 | bytes 4526080 | tf_op jit(solution)/shard_map/ijc,ch->hij/dot_general | solution.py:66
  21.3 12.0 %all_to_all.127 = f32[8,64,128]{2,1,0:T(8,128)S(1)} all-to-all(f32[8,64,128]{2,1,0:T(8,128)S(1)} %copy.129), channel_id=1, replica_groups=mesh['wide'=16,'narrow'=8] {'narrow'}, dimensions={0} | all-to-all | bytes 524288 | tf_op jit(solution)/shard_map/all_to_all | solution.py:69
  36.3 3.6 all-to-all-start.2
  41.6 6.1 %all-to-all-done.2 = f32[4,128,256]{1,0,2:T(4,128)S(1)} async-done(((f32[4,128,256]{1,0,2:T(4,128)}), f32[4,128,256]{1,0,2:T(4,128)S(1)}, u32[]{:S(2)}, u32[]{:S(2)}) %all-to-all-start.2) | async-done | bytes 524320 | tf_op jit(solution)/shard_map/all_to_all | solution.py:74
  47.7 3.5 all-to-all-start.1
  52.8 5.8 %all-to-all-done.1 = f32[4,128,256]{1,0,2:T(4,128)S(1)} async-done(((f32[4,128,256]{1,0,2:T(4,128)}), f32[4,128,256]{1,0,2:T(4,128)S(1)}, u32[]{:S(2)}, u32[]{:S(2)}) %all-to-all-start.1) | async-done | bytes 524320 | tf_op jit(solution)/shard_map/all_to_all | solution.py:73
  58.7 3.5 all-to-all-start
  63.8 5.8 %all-to-all-done = f32[4,128,256]{1,0,2:T(4,128)S(1)} async-done(((f32[4,128,256]{1,0,2:T(4,128)}), f32[4,128,256]{1,0,2:T(4,128)S(1)}, u32[]{:S(2)}, u32[]{:S(2)}) %all-to-all-start) | async-done | bytes 524320 | tf_op jit(solution)/shard_map/all_to_all | solution.py:72
  69.7 3.7 all-to-all-start.4
  79.3 7.6 %all-to-all-done.4 = f32[4,128,256]{1,0,2:T(4,128)S(1)} async-done(((f32[4,128,256]{1,0,2:T(4,128)}), f32[4,128,256]{1,0,2:T(4,128)S(1)}, u32[]{:S(2)}, u32[]{:S(2)}) %all-to-all-start.4) | async-done | bytes 524320 | tf_op jit(solution)/shard_map/all_to_all | solution.py:75
  87.9 9.7 %all-gather.2.cloned.1.call-done = f32[1,1024,1024]{2,0,1:T(1,128)} async-done(((f32[1,64,1024]{2,0,1:T(1,128)}), f32[1,1024,1024]{2,0,1:T(1,128)}) %all-gather.2.cloned.1.call-update) | async-done | bytes 4194320 | tf_op jit(solution)/shard_map/all_gather | solution.py:70
  97.6 5.2 %copy.134 = f32[1,1024,1024]{2,1,0:T(8,128)} copy(f32[1,1024,1024]{2,0,1:T(1,128)} %all-gather.2.cloned.1.call-done) | data formatting | bytes 8388608 | tf_op jit(solution)/shard_map/while | solution.py:107
  102.8 73.0 %while.31 = (s32[]{:T(128)}, f32[4,1024,32]{1,2,0:T(8,128)S(1)}, f32[4,1024,32]{2,1,0:T(8,128)}, f32[4,1024,32]{2,1,0:T(8,128)}, f32[4,1024,32]{2,1,0:T(8,128)},...) while((s32[]{:T(128)}, f32[4,1024,32]{1,2,0:T(8,128)S(1)}, ...), condition=%wide.region_9.10_spmd, body=%wide.region_4.9_spmd.sunk | while | flops 405797888 | bytes 10889644 | solution.py:107
  105.1 15.5 %while.33 = (s32[]{:T(128)}, f32[2,512,32]{1,2,0:T(8,128)S(1)}, s32[2]{0:T(128)S(1)}, f32[1024,1,32]{2,1,0:T(1,128)S(1)}, f32[1024,1,32]{2,1,0:T(1,128)S(1)}, /*...) while((s32[]{:T(128)}, f32[2,512,32]{1,2,0:T(8,128)S(1)}, ...), condition=%wide.region_8.8_spmd, body=%wide.region_5.7_spmd.sunk | while | flops 405797888 | bytes 9316539 | solution.py:104
  106.3 3.6 fusion.109
  114.1 3.6 fusion.109
  123.4 15.5 %while.33 = (s32[]{:T(128)}, f32[2,512,32]{1,2,0:T(8,128)S(1)}, s32[2]{0:T(128)S(1)}, f32[1024,1,32]{2,1,0:T(1,128)S(1)}, f32[1024,1,32]{2,1,0:T(1,128)S(1)}, /*...) while((s32[]{:T(128)}, f32[2,512,32]{1,2,0:T(8,128)S(1)}, ...), condition=%wide.region_8.8_spmd, body=%wide.region_5.7_spmd.sunk | while | flops 405797888 | bytes 9316539 | solution.py:104
  124.6 3.6 fusion.109
  132.3 3.6 fusion.109
  141.7 15.5 %while.33 = (s32[]{:T(128)}, f32[2,512,32]{1,2,0:T(8,128)S(1)}, s32[2]{0:T(128)S(1)}, f32[1024,1,32]{2,1,0:T(1,128)S(1)}, f32[1024,1,32]{2,1,0:T(1,128)S(1)}, /*...) while((s32[]{:T(128)}, f32[2,512,32]{1,2,0:T(8,128)S(1)}, ...), condition=%wide.region_8.8_spmd, body=%wide.region_5.7_spmd.sunk | while | flops 405797888 | bytes 9316539 | solution.py:104
  142.9 3.6 fusion.109
  147.0 2.4 fusion.111
  150.6 3.6 fusion.109
  159.9 15.5 %while.33 = (s32[]{:T(128)}, f32[2,512,32]{1,2,0:T(8,128)S(1)}, s32[2]{0:T(128)S(1)}, f32[1024,1,32]{2,1,0:T(1,128)S(1)}, f32[1024,1,32]{2,1,0:T(1,128)S(1)}, /*...) while((s32[]{:T(128)}, f32[2,512,32]{1,2,0:T(8,128)S(1)}, ...), condition=%wide.region_8.8_spmd, body=%wide.region_5.7_spmd.sunk | while | flops 405797888 | bytes 9316539 | solution.py:104
  161.1 3.6 fusion.109
  165.3 2.4 fusion.111
  168.9 3.6 fusion.109
  180.1 13.5 %all_to_all.128 = f32[8,1,16384]{2,1,0:T(1,128)S(1)} all-to-all(f32[8,1,16384]{2,1,0:T(1,128)S(1)} %reshape.149), channel_id=1, replica_groups=mesh['wide'=16,'narrow'=8] {'narrow'}, dimensions={0} | all-to-all | bytes 1048576 | tf_op jit(solution)/shard_map/all_to_all | solution.py:109
  201.8 11.7 %all_to_all.129 = f32[8,4,32,128]{3,2,1,0:T(8,128)S(1)} all-to-all(f32[8,4,32,128]{3,2,1,0:T(8,128)S(1)} %broadcast_in_dim.21), channel_id=1, replica_groups=mesh['wide'=16,'narrow'=8] {'narrow'}, dimensions={0} | all-to-all | bytes 1048576 | tf_op jit(solution)/shard_map/all_to_all | solution.py:19
  216.5 6.5 %all-to-all-start.7 = ((f32[16,1,8192]{2,1,0:T(1,128)}), f32[16,1,8192]{2,1,0:T(1,128)S(1)}, u32[]{:S(2)}, u32[]{:S(2)}) async-start(f32[16,1,8192]{2,1,0:T(1,128)} %reshape.151), calls=%async_computation.7 | async-start | bytes 1048576 | tf_op jit(solution)/shard_map/all_to_all | solution.py:121
  223.8 10.4 %all-to-all-done.7 = f32[16,1,8192]{2,1,0:T(1,128)S(1)} async-done(((f32[16,1,8192]{2,1,0:T(1,128)}), f32[16,1,8192]{2,1,0:T(1,128)S(1)}, u32[]{:S(2)}, u32[]{:S(2)}) %all-to-all-start.7) | async-done | bytes 524320 | tf_op jit(solution)/shard_map/all_to_all | solution.py:121
  235.4 5.3 %all-to-all-start.8 = ((f32[16,4,32,128]{3,1,2,0:T(4,128)}), f32[16,4,32,128]{3,1,2,0:T(4,128)}, u32[]{:S(2)}, u32[]{:S(2)}) async-start(f32[16,4,32,128]{3,1,2,0:T(4,128)} %broadcast_in_dim.22), calls=%async_computation.8 | async-start | bytes 2097152 | tf_op jit(solution)/shard_map/all_to_all | solution.py:19
  247.0 11.0 %all-to-all-done.8 = f32[16,4,32,128]{3,1,2,0:T(4,128)} async-done(((f32[16,4,32,128]{3,1,2,0:T(4,128)}), f32[16,4,32,128]{3,1,2,0:T(4,128)}, u32[]{:S(2)}, u32[]{:S(2)}) %all-to-all-start.8) | async-done | bytes 1048608 | tf_op jit(solution)/shard_map/all_to_all | solution.py:19
  260.0 96.4 %while.32 = (s32[]{:T(128)}, f32[4,16,128,128]{3,2,1,0:T(8,128)}, s32[4]{0:T(128)S(1)}, f32[64,32,64]{0,2,1:T(8,128)S(1)}, f32[64,32,128]{2,0,1:T(8,128)S(1)}, /...) while((s32[]{:T(128)}, f32[4,16,128,128]{3,2,1,0:T(8,128)}, ...), condition=%wide.region_13.14_spmd, body=%wide.region_12.13_spmd.sunk | while | flops 4833935360 | bytes 19660976 | solution.py:138
  261.3 6.8 %broadcast_multiply_fusion.6 = f32[32,16,32,128]{3,1,2,0:T(8,128)S(1)} fusion(f32[64,32,128]{2,0,1:T(8,128)S(1)} %get-tuple-element.440, f32[64,32,64]{0,2,1:T(8,128)S(1)} %get-tuple-element.439, s32[]{:T(128)S(6)} %select_n.9), kind=kOutput, calls=%fused_computation.17.clone.1 | convolution fusion | flops 1612709888 | bytes 9699332 | tf_op jit(solution)/shard_map/while/body/eval_jaxpr/sci,sdj->ijcd/dot_general | solution.py:132
  268.2 16.0 %fusion.104 = f32[4,16,128,128]{3,2,1,0:T(8,128)} fusion(f32[4,16,128,128]{3,2,1,0:T(8,128)} %get-tuple-element.427, s32[]{:T(128)S(6)} %copy.213, f32[16,128,1024]{1,0,2:T(8,128)S(1)} %bitcast.171, f32[1024,128]{1,0:T(8,128)S(1)} %get-tuple-element.441), kind=kOutput, calls=%fused_computation.19.clone.1 | convolution fusion | flops 3221225472 | bytes 9961476 | tf_op jit(solution)/shard_map/while/body/eval_jaxpr/dot_general | solution.py:34
  285.3 6.8 %broadcast_multiply_fusion.6 = f32[32,16,32,128]{3,1,2,0:T(8,128)S(1)} fusion(f32[64,32,128]{2,0,1:T(8,128)S(1)} %get-tuple-element.440, f32[64,32,64]{0,2,1:T(8,128)S(1)} %get-tuple-element.439, s32[]{:T(128)S(6)} %select_n.9), kind=kOutput, calls=%fused_computation.17.clone.1 | convolution fusion | flops 1612709888 | bytes 9699332 | tf_op jit(solution)/shard_map/while/body/eval_jaxpr/sci,sdj->ijcd/dot_general | solution.py:132
  292.1 16.0 %fusion.104 = f32[4,16,128,128]{3,2,1,0:T(8,128)} fusion(f32[4,16,128,128]{3,2,1,0:T(8,128)} %get-tuple-element.427, s32[]{:T(128)S(6)} %copy.213, f32[16,128,1024]{1,0,2:T(8,128)S(1)} %bitcast.171, f32[1024,128]{1,0:T(8,128)S(1)} %get-tuple-element.441), kind=kOutput, calls=%fused_computation.19.clone.1 | convolution fusion | flops 3221225472 | bytes 9961476 | tf_op jit(solution)/shard_map/while/body/eval_jaxpr/dot_general | solution.py:34
  309.2 6.8 %broadcast_multiply_fusion.6 = f32[32,16,32,128]{3,1,2,0:T(8,128)S(1)} fusion(f32[64,32,128]{2,0,1:T(8,128)S(1)} %get-tuple-element.440, f32[64,32,64]{0,2,1:T(8,128)S(1)} %get-tuple-element.439, s32[]{:T(128)S(6)} %select_n.9), kind=kOutput, calls=%fused_computation.17.clone.1 | convolution fusion | flops 1612709888 | bytes 9699332 | tf_op jit(solution)/shard_map/while/body/eval_jaxpr/sci,sdj->ijcd/dot_general | solution.py:132
  316.1 16.0 %fusion.104 = f32[4,16,128,128]{3,2,1,0:T(8,128)} fusion(f32[4,16,128,128]{3,2,1,0:T(8,128)} %get-tuple-element.427, s32[]{:T(128)S(6)} %copy.213, f32[16,128,1024]{1,0,2:T(8,128)S(1)} %bitcast.171, f32[1024,128]{1,0:T(8,128)S(1)} %get-tuple-element.441), kind=kOutput, calls=%fused_computation.19.clone.1 | convolution fusion | flops 3221225472 | bytes 9961476 | tf_op jit(solution)/shard_map/while/body/eval_jaxpr/dot_general | solution.py:34
  333.2 6.8 %broadcast_multiply_fusion.6 = f32[32,16,32,128]{3,1,2,0:T(8,128)S(1)} fusion(f32[64,32,128]{2,0,1:T(8,128)S(1)} %get-tuple-element.440, f32[64,32,64]{0,2,1:T(8,128)S(1)} %get-tuple-element.439, s32[]{:T(128)S(6)} %select_n.9), kind=kOutput, calls=%fused_computation.17.clone.1 | convolution fusion | flops 1612709888 | bytes 9699332 | tf_op jit(solution)/shard_map/while/body/eval_jaxpr/sci,sdj->ijcd/dot_general | solution.py:132
  340.0 16.0 %fusion.104 = f32[4,16,128,128]{3,2,1,0:T(8,128)} fusion(f32[4,16,128,128]{3,2,1,0:T(8,128)} %get-tuple-element.427, s32[]{:T(128)S(6)} %copy.213, f32[16,128,1024]{1,0,2:T(8,128)S(1)} %bitcast.171, f32[1024,128]{1,0:T(8,128)S(1)} %get-tuple-element.441), kind=kOutput, calls=%fused_computation.19.clone.1 | convolution fusion | flops 3221225472 | bytes 9961476 | tf_op jit(solution)/shard_map/while/body/eval_jaxpr/dot_general | solution.py:34
  356.4 4.6 %fusion.80 = (f32[64,128]{1,0:T(8,128)S(1)}, f32[64,128,128]{2,1,0:T(8,128)S(1)}) fusion(f32[128]{0:T(128)S(1)} %copy-done.18, f32[64,128,128]{2,1,0:T(8,128)} %param.24, f32[4,16,128,128]{3,2,1,0:T(8,128)} %get-tuple-element.104), kind=kLoop, calls=%fused_computation.97 | loop fusion | flops 3137536 | bytes 12616192 | tf_op jit(solution)/shard_map/reduce_sum | solution.py:27
  361.1 2.6 multiply_reduce_fusion
  363.8 13.4 %fusion.31 = f32[64,128,512]{2,1,0:T(8,128)S(1)} fusion(f32[64,128,128]{2,1,0:T(8,128)S(1)} %get-tuple-element.198, f32[64,128]{1,0:T(8,128)S(1)} %add_rsqrt_fusion, f32[64,128]{1,0:T(8,128)S(1)} %broadcast_multiply_fusion.1, f32[128,512]{1,0:T(8,128)S(1)} %copy-done), kind=kOutput, calls=%fused_computation.32 | convolution fusion | flops 6444548096 | bytes 21299200 | tf_op jit(solution)/shard_map/dot_general | solution.py:34
  377.2 14.8 %fusion.41 = f32[64,128,128]{2,1,0:T(8,128)} fusion(f32[64,128,128]{2,1,0:T(8,128)S(1)} %get-tuple-element.198, f32[64,128,512]{2,1,0:T(8,128)S(1)} %fusion.31, f32[512]{0:T(512)S(1)} %copy-done.15, f32[512,128]{1,0:T(8,128)S(1)} %copy-done.7), kind=kOutput, calls=%fused_computation.44 | convolution fusion | flops 6451888128 | bytes 25430016 | tf_op jit(solution)/shard_map/dot_general | solution.py:34
  (154 shorter events, 77.2 us)
Async XLA Ops:
  7.2 356.6 %copy-start = (f32[128,512]{1,0:T(8,128)S(1)}, f32[128,512]{1,0:T(8,128)}, u32[]{:S(2)}) copy-start(f32[128,512]{1,0:T(8,128)} %param.37) | copy-start | bytes 786436
  7.2 7.6 %copy-start.14 = (f32[128,8]{0,1:T(8,128)S(1)}, f32[128,8]{0,1:T(8,128)}, u32[]{:S(2)}) copy-start(f32[128,8]{0,1:T(8,128)} %param.30) | copy-start | bytes 12292
  7.2 90.4 %all-gather.2.cloned.1.call-start = ((), (), s32[]{:S(2)}) async-start(), calls=%async_computation.9 | async-start | bytes 4456448 | tf_op jit(solution)/shard_map/all_gather | solution.py:70
  10.6 4.2 %copy-start.1 = (f32[64,128,128]{2,1,0:T(8,128)S(1)}, f32[64,128,128]{2,1,0:T(8,128)}, u32[]{:S(2)}) copy-start(f32[64,128,128]{2,1,0:T(8,128)} %param.24) | copy-start | bytes 12582916
  14.8 19.5 %copy-start.2 = (f32[4,128,256]{2,1,0:T(8,128)S(1)}, f32[4,128,256]{2,1,0:T(8,128)}, u32[]{:S(2)}) copy-start(f32[4,128,256]{2,1,0:T(8,128)} %param.23) | copy-start | bytes 1572868
  14.8 19.9 %copy-start.8 = (f32[256,256]{1,0:T(8,128)S(1)}, f32[256,256]{1,0:T(8,128)}, u32[]{:S(2)}) copy-start(f32[256,256]{1,0:T(8,128)} %param.27) | copy-start | bytes 786436
  21.2 18.7 %copy-start.9 = (f32[256,256]{1,0:T(8,128)S(1)}, f32[256,256]{1,0:T(8,128)}, u32[]{:S(2)}) copy-start(f32[256,256]{1,0:T(8,128)} %param.26) | copy-start | bytes 786436
  34.2 17.0 %copy-start.10 = (f32[256,256]{1,0:T(8,128)S(1)}, f32[256,256]{1,0:T(8,128)}, u32[]{:S(2)}) copy-start(f32[256,256]{1,0:T(8,128)} %param.25) | copy-start | bytes 786436
  36.3 25.9 %copy-start.11 = (f32[256,256]{1,0:T(8,128)S(1)}, f32[256,256]{1,0:T(8,128)}, u32[]{:S(2)}) copy-start(f32[256,256]{1,0:T(8,128)} %param.28) | copy-start | bytes 786436
  36.3 25.9 %copy-start.17 = (f32[256]{0:T(256)S(1)}, f32[256]{0:T(256)}, u32[]{:S(2)}) copy-start(f32[256]{0:T(256)} %param.29) | copy-start | bytes 3076
  36.3 11.4 %all-to-all-start.2 = ((f32[4,128,256]{1,0,2:T(4,128)}), f32[4,128,256]{1,0,2:T(4,128)S(1)}, u32[]{:S(2)}, u32[]{:S(2)}) async-start(f32[4,128,256]{1,0,2:T(4,128)} %copy.126), calls=%async_computation.2 | async-start | bytes 1048576 | tf_op jit(solution)/shard_map/all_to_all | solution.py:74
  47.7 11.0 %all-to-all-start.1 = ((f32[4,128,256]{1,0,2:T(4,128)}), f32[4,128,256]{1,0,2:T(4,128)S(1)}, u32[]{:S(2)}, u32[]{:S(2)}) async-start(f32[4,128,256]{1,0,2:T(4,128)} %copy.123), calls=%async_computation.1 | async-start | bytes 1048576 | tf_op jit(solution)/shard_map/all_to_all | solution.py:73
  58.7 11.0 %all-to-all-start = ((f32[4,128,256]{1,0,2:T(4,128)}), f32[4,128,256]{1,0,2:T(4,128)S(1)}, u32[]{:S(2)}, u32[]{:S(2)}) async-start(f32[4,128,256]{1,0,2:T(4,128)} %copy.120), calls=%async_computation | async-start | bytes 1048576 | tf_op jit(solution)/shard_map/all_to_all | solution.py:72
  69.7 17.2 %all-to-all-start.4 = ((f32[4,128,256]{1,0,2:T(4,128)}), f32[4,128,256]{1,0,2:T(4,128)S(1)}, u32[]{:S(2)}, u32[]{:S(2)}) async-start(f32[4,128,256]{1,0,2:T(4,128)} %copy.135), calls=%async_computation.4 | async-start | bytes 1048576 | tf_op jit(solution)/shard_map/all_to_all | solution.py:75
  87.9 14.9 %copy-start.5 = (f32[4,1024,32]{1,2,0:T(8,128)S(1)}, f32[4,1024,32]{1,2,0:T(8,128)}, u32[]{:S(2)}) copy-start(f32[4,1024,32]{1,2,0:T(8,128)} %custom-call.1) | copy-start | bytes 1572868
  175.8 0.8 copy-start.6
  180.1 18.5 %copy-start.16 = (f32[256]{0:T(256)S(1)}, f32[256]{0:T(256)}, u32[]{:S(2)}) copy-start(f32[256]{0:T(256)} %param.32) | copy-start | bytes 3076
  194.2 6.9 %copy-start.12 = (f32[256,32]{0,1:T(8,128)S(1)}, f32[256,32]{0,1:T(8,128)}, u32[]{:S(2)}) copy-start(f32[256,32]{0,1:T(8,128)} %param.33) | copy-start | bytes 98308
  200.7 22.2 %copy-start.4 = (f32[4,128,256]{2,1,0:T(8,128)}, f32[4,128,256]{2,1,0:T(8,128)S(1)}, u32[]{:S(2)}) copy-start(f32[4,128,256]{2,1,0:T(8,128)S(1)} %get-tuple-element.204) | copy-start | bytes 1572868
  201.0 22.0 %copy-start.13 = (f32[256,32]{0,1:T(8,128)S(1)}, f32[256,32]{0,1:T(8,128)}, u32[]{:S(2)}) copy-start(f32[256,32]{0,1:T(8,128)} %param.34) | copy-start | bytes 98308
  216.5 17.6 %all-to-all-start.7 = ((f32[16,1,8192]{2,1,0:T(1,128)}), f32[16,1,8192]{2,1,0:T(1,128)S(1)}, u32[]{:S(2)}, u32[]{:S(2)}) async-start(f32[16,1,8192]{2,1,0:T(1,128)} %reshape.151), calls=%async_computation.7 | async-start | bytes 1048576 | tf_op jit(solution)/shard_map/all_to_all | solution.py:121
  235.4 22.6 %all-to-all-start.8 = ((f32[16,4,32,128]{3,1,2,0:T(4,128)}), f32[16,4,32,128]{3,1,2,0:T(4,128)}, u32[]{:S(2)}, u32[]{:S(2)}) async-start(f32[16,4,32,128]{3,1,2,0:T(4,128)} %broadcast_in_dim.22), calls=%async_computation.8 | async-start | bytes 2097152 | tf_op jit(solution)/shard_map/all_to_all | solution.py:19
  243.6 16.4 %copy-start.3 = (f32[1024,128]{1,0:T(8,128)S(1)}, f32[1024,128]{1,0:T(8,128)}, u32[]{:S(2)}) copy-start(f32[1024,128]{1,0:T(8,128)} %param.35) | copy-start | bytes 1572868
  260.0 96.4 %copy-start.18 = (f32[128]{0:T(128)S(1)}, f32[128]{0:T(128)}, u32[]{:S(2)}) copy-start(f32[128]{0:T(128)} %param.36) | copy-start | bytes 1540
  363.7 13.5 %copy-start.7 = (f32[512,128]{1,0:T(8,128)S(1)}, f32[512,128]{1,0:T(8,128)}, u32[]{:S(2)}) copy-start(f32[512,128]{1,0:T(8,128)} %param.39) | copy-start | bytes 786436
  363.8 13.5 %copy-start.15 = (f32[512]{0:T(512)S(1)}, f32[512]{0:T(512)}, u32[]{:S(2)}) copy-start(f32[512]{0:T(512)} %param.38) | copy-start | bytes 6148
Sparse Core Ops, SparseCore 0:
  34.4 63.1 all-gather.1
where the time goes:
time: 406 us; the launch traced here: 399 us
  matrix products  180 us (44%)
  waiting for transfers between devices  56.4 us (14%)
  local copies, waits for them, and re-layouts  51.2 us (13%)
  blocking collectives  37.2 us (9%)
  starting transfers between devices  26.1 us (6%)
  other arithmetic  25.4 us (6%)
  between operations  14.8 us (4%)
  loops' own time  7.86 us (2%)
    dot_general x11, matrix products, matrix_multiply(): jnp.dot(first_arr, second_arr, precision=finest_precision, preferred_elem...  96.8 us
    dot_general x8, matrix products, per_block(): jnp.einsum('qhd,khd->hqk', query_rows, key_item, precision=finest_precision)  28.9 us
    dot_general x4, matrix products, outer_block(): jnp.einsum('sci,sdj->ijcd', left_part, right_all, precision=finest_precis...  27.3 us
    dot_general x8, matrix products, per_block(): jnp.einsum('hqk,khd->qhd', softmax_probabilities, value_item, precision=f...  19.2 us
    all_to_all x1, blocking collectives, per_device(): lax.all_to_all(outcome, 'narrow', split_axis=1, concat_axis=2, tiled=True)  13.5 us
    all_to_all x1, blocking collectives, per_device(): lax.all_to_all(bias_tile, 'narrow', split_axis=0, concat_axis=2, tiled=True)  12 us
    all_to_all x1, blocking collectives, copy_for_each(): lax.all_to_all(jnp.broadcast_to(x[None], (devices, *x.shape)), axis, 0, 0...  11.7 us
    while x4, local copies, waits for them, and re-layouts, per_device(): outcome = lax.map(per_item, (operands[0], operands[1], operands[2]))  11.1 us
  transfers between devices with their start and end apart: 7, of which 7 were waited for; matrix products, arithmetic and copies ran while one was open for 5% of the time, Pallas kernels for 0%

commit v1 on v0

v1 whole, which is shorter than its diff:
```python
import functools
import math

import jax
import jax.numpy as jnp
from jax import lax
from jax.experimental import pallas as pl
from jax.experimental.pallas import tpu as pltpu
from jax.sharding import PartitionSpec as P

F32 = jnp.float32
BF16 = jnp.bfloat16
LOG2E = math.log2(math.e)
VMEM_LIMIT = 60 * 1024 * 1024
MESH = pl.DeviceIdType.MESH

NT = (((1,), (1,)), ((), ()))


def dot(a, b):
    return jnp.dot(a, b, preferred_element_type=F32)


def split(x):
    hi = x.astype(BF16)
    lo = (x - hi.astype(F32)).astype(BF16)
    return hi, lo


def split32(x):
    hi = x.astype(BF16).astype(F32)
    return hi, (x - hi).astype(BF16).astype(F32)


def dot3(a_hi, a_lo, b_hi, b_lo):
    return dot(a_hi, b_hi) + dot(a_hi, b_lo) + dot(a_lo, b_hi)


def normalize(x):
    mean = jnp.mean(x, axis=-1, keepdims=True)
    centered = x - mean
    variance = jnp.mean(centered * centered, axis=-1, keepdims=True)
    return centered * lax.rsqrt(variance + 1e-5)


def whole(memory_space=pltpu.VMEM):
    return pl.BlockSpec(memory_space=memory_space)


def full(shape):
    return pl.BlockSpec(shape, lambda *_: (0,) * len(shape))


def bias_kernel(pair_ref, weight_ref, out_ref):
    rows, cols, channels = pair_ref.shape
    heads = weight_ref.shape[0]
    normed = normalize(pair_ref[...].reshape(rows * cols, channels))
    n_hi, n_lo = split(normed)
    stacked = jnp.concatenate([n_hi, n_lo], axis=1)
    w_hi, w_lo = split32(weight_ref[...] * LOG2E)
    top = jnp.concatenate([w_hi, w_hi], axis=1)
    low = jnp.concatenate([w_lo, jnp.zeros_like(w_lo)], axis=1)
    weights = jnp.concatenate([top, low], axis=0).astype(BF16)
    both = lax.dot_general(weights, stacked, NT, preferred_element_type=F32)
    result = both[:heads] + both[heads:]
    for row in range(rows):
        out_ref[:, row, :] = result[:, row * cols : (row + 1) * cols]


def pair_bias(pair_state, weight_t):
    rows, cols, channels = pair_state.shape
    heads = weight_t.shape[0]
    step = 8
    return pl.pallas_call(
        bias_kernel,
        grid=(rows // step,),
        in_specs=[
            pl.BlockSpec((step, cols, channels), lambda i: (i, 0, 0)),
            full((heads, channels)),
        ],
        out_specs=pl.BlockSpec((heads, step, cols), lambda i: (0, i, 0)),
        out_shape=jax.ShapeDtypeStruct((heads, rows, cols), F32),
        compiler_params=pltpu.CompilerParams(vmem_limit_bytes=VMEM_LIMIT),
        name="pair_bias",
    )(pair_state, weight_t)


def project_kernel(x_ref, q_ref, k_ref, v_ref, g_ref, off_ref, out_ref, gate_ref):
    seqs, res, channels = x_ref.shape
    heads = out_ref.shape[0]
    width = channels // heads
    per_tile = 128 // width
    normed = normalize(x_ref[...].reshape(seqs * res, channels))
    n_hi, n_lo = split(normed)
    scale = LOG2E / math.sqrt(width)
    for kind, ref in enumerate((q_ref, k_ref, v_ref)):
        w_hi, w_lo = split(ref[...])
        y = dot3(n_hi, n_lo, w_hi, w_lo)
        if kind == 0:
            y = y * scale
        for s in range(seqs):
            for tile in range(channels // 128):
                part = y[s * res : (s + 1) * res, tile * 128 : (tile + 1) * 128].T
                for h in range(per_tile):
                    out_ref[tile * per_tile + h, s, kind * width : (kind + 1) * width, :] = part[
                        h * width : (h + 1) * width
                    ]
    w_hi, w_lo = split(g_ref[...])
    gate = jax.nn.sigmoid(dot3(n_hi, n_lo, w_hi, w_lo) + off_ref[...])
    gate_ref[...] = gate.reshape(seqs, res, channels)


def project(x, wq, wk, wv, wg, offset, heads):
    seqs, res, channels = x.shape
    width = channels // heads
    return pl.pallas_call(
        project_kernel,
        in_specs=[whole()] * 6,
        out_specs=[whole(), whole()],
        out_shape=[
            jax.ShapeDtypeStruct((heads, seqs, 3 * width, res), F32),
            jax.ShapeDtypeStruct((seqs, res, channels), F32),
        ],
        compiler_params=pltpu.CompilerParams(vmem_limit_bytes=VMEM_LIMIT),
        name="project",
    )(x, wq, wk, wv, wg, offset.reshape(1, channels))


def place(wide, narrow):
    return {"wide": wide, "narrow": narrow}


def greet(peers):
    barrier = pltpu.get_barrier_semaphore()
    for peer in peers:
        pl.semaphore_signal(barrier, inc=1, device_id=peer, device_id_type=MESH)
    pl.semaphore_wait(barrier, len(peers))


def remote(src, dst, send, recv, peer):
    return pltpu.make_async_remote_copy(
        src_ref=src, dst_ref=dst, send_sem=send, recv_sem=recv, device_id=peer, device_id_type=MESH
    )


def wide_links(wide):
    z, x, core = wide // 4, (wide // 2) % 2, wide % 2
    at = lambda z_, x_, c_: (z_ * 2 + x_) * 2 + c_
    up, down, far = (z + 1) % 4, (z + 3) % 4, (z + 2) % 4
    return z, x, core, at, up, down, far


def gather_wide(buf, rows, send, recv):
    wide, narrow = lax.axis_index("wide"), lax.axis_index("narrow")
    z, x, core, at, up, down, far = wide_links(wide)
    other_x, other_core = 1 - x, 1 - core
    half = rows // 2

    def slab(z_, x_, c_, part=None):
        start = at(z_, x_, c_) * rows
        if part is None:
            return buf.at[pl.ds(start, rows)]
        return buf.at[pl.ds(start + part * half, half)]

    up_dev = place(at(up, x, core), narrow)
    down_dev = place(at(down, x, core), narrow)
    x_dev = place(at(z, other_x, core), narrow)
    core_dev = place(at(z, x, other_core), narrow)
    started = []
    count = [0]

    def push(region, index, dev):
        copy = remote(region, region, send.at[index], recv.at[index], dev)
        copy.start()
        started.append(copy)

    def arrived(region, index):
        remote(region, region, send.at[index], recv.at[index], core_dev).wait_recv()

    own = slab(z, x, core)
    push(own, 1, up_dev)
    push(own, 2, down_dev)
    push(own, 0, x_dev)
    push(own, 9, core_dev)
    expected = [(slab(z, x, other_core), 9)]

    def side(s, x_):
        below, above = slab(down, x_, core), slab(up, x_, core)
        base = 1 + 4 * s
        arrived(below, base)
        push(slab(down, x_, core, 0), base + 2, up_dev)
        push(below, 9 + base, core_dev)
        arrived(above, base + 1)
        push(slab(up, x_, core, 1), base + 3, down_dev)
        push(above, 9 + base + 1, core_dev)

    def finish(s, x_):
        base = 1 + 4 * s
        for part in range(2):
            region = slab(far, x_, core, part)
            arrived(region, base + 2 + part)
            push(region, 9 + base + 2 + part, core_dev)

    def partner(s, x_):
        base = 9 + 1 + 4 * s
        expected.append((slab(down, x_, other_core), base))
        expected.append((slab(up, x_, other_core), base + 1))
        for part in range(2):
            expected.append((slab(far, x_, other_core, part), base + 2 + part))

    cross = slab(z, other_x, core)
    arrived(cross, 0)
    push(cross, 5, up_dev)
    push(cross, 6, down_dev)
    push(cross, 18, core_dev)
    expected.append((slab(z, other_x, other_core), 18))
    side(0, x)
    finish(0, x)
    side(1, other_x)
    finish(1, other_x)
    partner(0, x)
    partner(1, other_x)
    for region, index in expected:
        arrived(region, index)
    for copy in started:
        copy.wait_send()


def wide_peers():
    wide, narrow = lax.axis_index("wide"), lax.axis_index("narrow")
    z, x, core, at, up, down, far = wide_links(wide)
    return [
        place(at(up, x, core), narrow),
        place(at(down, x, core), narrow),
        place(at(z, 1 - x, core), narrow),
        place(at(z, x, 1 - core), narrow),
    ]


def narrow_peers():
    wide, narrow = lax.axis_index("wide"), lax.axis_index("narrow")
    return [place(wide, narrow ^ k) for k in range(1, 8)]


def heads_kernel(qkv, bias, qkv_out, bias_out, local, b_send, b_recv, q_send, q_recv, send, recv):
    wide, narrow = lax.axis_index("wide"), lax.axis_index("narrow")
    rows, cols = bias.shape[1:]
    greet(narrow_peers() + wide_peers())

    def bias_slot(source):
        return bias_out.at[pl.ds(wide * rows, rows), pl.ds(source * cols, cols)]

    own_bias = pltpu.make_async_copy(bias.at[narrow], bias_slot(narrow), local.at[0])
    own_bias.start()
    copies = []
    for k in range(1, 8):
        peer = narrow ^ k
        copy = remote(
            bias.at[peer], bias_slot(narrow), b_send.at[k], b_recv.at[k], place(wide, peer)
        )
        copy.start()
        copies.append(copy)
    own_qkv = pltpu.make_async_copy(qkv.at[narrow], qkv_out.at[narrow], local.at[1])
    own_qkv.start()
    for k in range(1, 8):
        peer = narrow ^ k
        copy = remote(
            qkv.at[peer], qkv_out.at[narrow], q_send.at[k], q_recv.at[k], place(wide, peer)
        )
        copy.start()
        copies.append(copy)
    own_bias.wait()
    for k in range(1, 8):
        slot = bias_slot(narrow ^ k)
        remote(slot, slot, b_send.at[k], b_recv.at[k], place(wide, narrow ^ k)).wait_recv()
    gather_wide(bias_out, rows, send, recv)
    for k in range(1, 8):
        slot = qkv_out.at[narrow ^ k]
        remote(slot, slot, q_send.at[k], q_recv.at[k], place(wide, narrow ^ k)).wait_recv()
    own_qkv.wait()
    for copy in copies:
        copy.wait_send()


DMA = pltpu.SemaphoreType.DMA


def exchange_heads(qkv, bias, wide_size):
    heads, rows, cols = bias.shape
    return pl.pallas_call(
        heads_kernel,
        in_specs=[whole(), whole()],
        out_specs=[whole(pl.ANY), whole(pl.ANY)],
        out_shape=[
            jax.ShapeDtypeStruct(qkv.shape, F32),
            jax.ShapeDtypeStruct((wide_size * rows, heads * cols), F32),
        ],
        scratch_shapes=[DMA((2,)), DMA((8,)), DMA((8,)), DMA((8,)), DMA((8,)), DMA((19,)), DMA((19,))],
        compiler_params=pltpu.CompilerParams(
            collective_id=0, has_side_effects=True, vmem_limit_bytes=VMEM_LIMIT
        ),
        name="exchange_heads",
    )(qkv, bias)


def swap_kernel(src, out, local, send, recv):
    wide, narrow = lax.axis_index("wide"), lax.axis_index("narrow")
    greet(narrow_peers())
    copies = []
    for k in range(1, 8):
        peer = narrow ^ k
        copy = remote(src.at[peer], out.at[narrow], send.at[k], recv.at[k], place(wide, peer))
        copy.start()
        copies.append(copy)
    own = pltpu.make_async_copy(src.at[narrow], out.at[narrow], local)
    own.start()
    for k in range(1, 8):
        slot = out.at[narrow ^ k]
        remote(slot, slot, send.at[k], recv.at[k], place(wide, narrow ^ k)).wait_recv()
    own.wait()
    for copy in copies:
        copy.wait_send()


def exchange_back(src):
    return pl.pallas_call(
        swap_kernel,
        in_specs=[whole()],
        out_specs=whole(pl.ANY),
        out_shape=jax.ShapeDtypeStruct(src.shape, F32),
        scratch_shapes=[DMA, DMA((8,)), DMA((8,))],
        compiler_params=pltpu.CompilerParams(
            collective_id=1, has_side_effects=True, vmem_limit_bytes=VMEM_LIMIT
        ),
        name="exchange_back",
    )(src)


def factors_kernel(left, right, left_out, right_out, local, l_send, l_recv, send, recv):
    wide, narrow = lax.axis_index("wide"), lax.axis_index("narrow")
    seqs = right.shape[0]
    barrier = pltpu.get_barrier_semaphore()
    source_narrow = wide // 2
    for w in range(16):
        me = jnp.logical_and(wide == w, narrow == source_narrow)

        @pl.when(jnp.logical_not(me))
        def _():
            pl.semaphore_signal(
                barrier, inc=1, device_id=place(w, source_narrow), device_id_type=MESH
            )

    for peer in wide_peers():
        pl.semaphore_signal(barrier, inc=1, device_id=peer, device_id_type=MESH)
    selfish = (wide // 2) == narrow
    pl.semaphore_wait(barrier, 2 * 8 - selfish.astype(jnp.int32) + 4)

    own_right = pltpu.make_async_copy(right, right_out.at[pl.ds(wide * seqs, seqs)], local.at[0])
    own_right.start()

    def target(half, k):
        return 2 * narrow + half, narrow ^ k

    def left_copy(half, k):
        w, n = target(half, k)
        return remote(
            left.at[half], left_out.at[wide], l_send.at[half, k], l_recv.at[wide], place(w, n)
        )

    own_left = pltpu.make_async_copy(left.at[wide % 2], left_out.at[wide], local.at[1])
    for k in range(8):
        for half in range(2):
            me = jnp.logical_and(selfish, wide % 2 == half) if k == 0 else None
            if me is None:
                left_copy(half, k).start()
            else:

                @pl.when(jnp.logical_not(me))
                def _():
                    left_copy(half, k).start()

                @pl.when(me)
                def _():
                    own_left.start()

    own_right.wait()
    gather_wide(right_out, seqs, send, recv)

    for w in range(16):
        me = jnp.logical_and(selfish, wide == w)

        @pl.when(jnp.logical_not(me))
        def _():
            slot = left_out.at[w]
            remote(
                slot, slot, l_send.at[0, 0], l_recv.at[w], place(w, source_narrow)
            ).wait_recv()

    @pl.when(selfish)
    def _():
        own_left.wait()

    for k in range(8):
        for half in range(2):
            if k:
                left_copy(half, k).wait_send()
            else:
                me = jnp.logical_and(selfish, wide % 2 == half)

                @pl.when(jnp.logical_not(me))
                def _():
                    left_copy(half, k).wait_send()


def exchange_factors(left, right, wide_size):
    return pl.pallas_call(
        factors_kernel,
        in_specs=[whole(), whole()],
        out_specs=[whole(pl.ANY), whole(pl.ANY)],
        out_shape=[
            jax.ShapeDtypeStruct((wide_size, *left.shape[1:]), F32),
            jax.ShapeDtypeStruct((wide_size * right.shape[0], *right.shape[1:]), F32),
        ],
        scratch_shapes=[DMA((2,)), DMA((2, 8)), DMA((16,)), DMA((19,)), DMA((19,))],
        compiler_params=pltpu.CompilerParams(
            collective_id=2, has_side_effects=True, vmem_limit_bytes=VMEM_LIMIT
        ),
        name="exchange_factors",
    )(left, right)


def attention_kernel(qkv_ref, bias_ref, out_ref, q_s, k_s, v_s, w_s):
    blocks, seqs, stacked, res = qkv_ref.shape
    width = stacked // 3

    @pl.when(pl.program_id(0) == 0)
    def _():
        pad = jnp.zeros((width, res), F32)
        for s in range(seqs):
            for b in range(blocks):
                cols = slice(b * res, (b + 1) * res)
                q_hi, q_lo = split32(qkv_ref[b, s, 0:width, :])
                k_hi, k_lo = split32(qkv_ref[b, s, width : 2 * width, :])
                v_hi, v_lo = split32(qkv_ref[b, s, 2 * width :, :])
                q_s[s, cols, :] = jnp.concatenate([q_hi, q_hi, q_lo, q_lo], axis=0).T.astype(BF16)
                k_s[s, :, cols] = jnp.concatenate([k_hi, k_lo, k_hi, k_lo], axis=0).astype(BF16)
                one = jnp.ones_like(pad)
                v_s[s, cols, :] = jnp.concatenate([v_hi, v_lo, one, pad], axis=0).T.astype(BF16)
                w_s[s, cols, :] = jnp.concatenate([v_hi, pad, one, pad], axis=0).T.astype(BF16)

    block = pl.program_id(0)
    bias = bias_ref[...]
    start = pl.multiple_of(block * res, res)
    for s in range(seqs):
        scores = dot(q_s[s, pl.ds(start, res), :], k_s[s]) + bias
        top = jnp.max(scores, axis=-1, keepdims=True)
        weights = jnp.exp2(scores - top)
        p_hi, p_lo = split(weights)
        mixed = (dot(p_hi, v_s[s]) + dot(p_lo, w_s[s])).T
        out_ref[0, s] = (mixed[:width] + mixed[width : 2 * width]) / mixed[2 * width : 3 * width]


def attention(qkv, bias):
    blocks, seqs, stacked, res = qkv.shape
    width = stacked // 3
    span = blocks * res
    return pl.pallas_call(
        attention_kernel,
        grid=(blocks,),
        in_specs=[full(qkv.shape), pl.BlockSpec((res, span), lambda i: (i, 0))],
        out_specs=pl.BlockSpec((1, seqs, width, res), lambda i: (i, 0, 0, 0)),
        out_shape=jax.ShapeDtypeStruct((blocks, seqs, width, res), F32),
        scratch_shapes=[
            pltpu.VMEM((seqs, span, 4 * width), BF16),
            pltpu.VMEM((seqs, 4 * width, span), BF16),
            pltpu.VMEM((seqs, span, 4 * width), BF16),
            pltpu.VMEM((seqs, span, 4 * width), BF16),
        ],
        compiler_params=pltpu.CompilerParams(vmem_limit_bytes=VMEM_LIMIT),
        name="attention",
    )(qkv, bias)


def mix_kernel(o_ref, gate_ref, x_ref, w_ref, off_ref, f_ref, s_ref, next_ref, left_ref, right_ref):
    heads, seqs, width, res = o_ref.shape
    channels = heads * width
    w_hi, w_lo = split(w_ref[...])
    pieces = []
    for s in range(seqs):
        stacked = o_ref[:, s].reshape(channels, res)
        pieces.append(stacked.T)
    attended = jnp.concatenate(pieces, axis=0) * gate_ref[...].reshape(seqs * res, channels)
    a_hi, a_lo = split(attended)
    x = x_ref[...].reshape(seqs * res, channels)
    after = x + dot3(a_hi, a_lo, w_hi, w_lo) + off_ref[...]
    next_ref[...] = after.reshape(seqs, res, channels)
    n_hi, n_lo = split(normalize(after))
    first = f_ref[...]
    factors = jnp.concatenate([first] * 4 + [s_ref[...]] * 4, axis=1)
    f_hi, f_lo = split(factors)
    y = dot3(n_hi, n_lo, f_hi, f_lo)
    hidden = first.shape[1]
    quarter = lax.broadcasted_iota(jnp.int32, (res // 8, 128), 1) // hidden
    for s in range(seqs):
        left = y[s * res : (s + 1) * res, :128]
        for half in range(2):
            rows = left[half * res // 2 : (half + 1) * res // 2].reshape(4, res // 8, 128)
            picked = rows[0]
            for q in range(1, 4):
                picked = jnp.where(quarter == q, rows[q], picked)
            left_ref[half, s] = picked
        right_ref[s] = y[s * res : (s + 1) * res, 128:].T[:hidden]


def mix(o, gate, x, w, offset, first, second):
    seqs, res, channels = x.shape
    hidden = first.shape[1]
    return pl.pallas_call(
        mix_kernel,
        in_specs=[whole()] * 7,
        out_specs=[whole()] * 3,
        out_shape=[
            jax.ShapeDtypeStruct(x.shape, F32),
            jax.ShapeDtypeStruct((2, seqs, res // 8, 128), F32),
            jax.ShapeDtypeStruct((seqs, hidden, res), F32),
        ],
        compiler_params=pltpu.CompilerParams(vmem_limit_bytes=VMEM_LIMIT),
        name="mix",
    )(o, gate, x, w, offset.reshape(1, channels), first, second)


def pair_kernel(
    left_ref, right_ref, pair_ref, w_ref, ob_ref, up_ref, eb_ref, down_ref, out_ref,
    l_s, r_s, wt_s, u_s, d_s, oh_s, ol_s,
):
    seqs, groups, _ = left_ref.shape
    hidden, cols = right_ref.shape[1:]
    channels = pair_ref.shape[-1]
    span = hidden * hidden

    @pl.when(pl.program_id(0) == 0)
    def _():
        for r in range(groups):
            hi, lo = split32(left_ref[:, r, :])
            l_s[r * 128 : (r + 1) * 128, 0:128] = jnp.concatenate([hi, hi], axis=0).T.astype(BF16)
            l_s[r * 128 : (r + 1) * 128, 128:256] = jnp.concatenate([lo, lo], axis=0).T.astype(BF16)
        for d in range(hidden):
            hi, lo = split(right_ref[:, d, :])
            part = slice(d * cols, (d + 1) * cols)
            r_s[:, part] = jnp.concatenate([hi, lo, hi, lo], axis=0)
        for b in range(span // 128):
            rows = [w_ref[pl.ds(b * 4 + e, hidden, stride=hidden), :] for e in range(4)]
            w_hi, w_lo = split32(jnp.concatenate(rows, axis=0).T)
            wt_s[0:channels, b * 128 : (b + 1) * 128] = w_hi.astype(BF16)
            wt_s[channels : 2 * channels, b * 128 : (b + 1) * 128] = w_lo.astype(BF16)
        u_hi, u_lo = split(up_ref[...])
        u_s[0:channels] = u_hi
        u_s[channels : 2 * channels] = u_hi
        u_s[2 * channels :] = u_lo
        d_hi, d_lo = split(down_ref[...])
        d_s[:, 0:channels] = d_hi
        d_s[:, channels:] = d_lo

    step = pl.program_id(0)
    lhs = l_s[pl.ds(pl.multiple_of(step * 256, 256), 256), :]
    for d2 in range(hidden // 2):
        o_hi, o_lo = split(dot(lhs, r_s[:, d2 * 2 * cols : (d2 + 1) * 2 * cols]))
        for r2 in range(2):
            for q in range(4):
                rows = slice((r2 * 4 + q) * hidden, (r2 * 4 + q + 1) * hidden)
                for e in range(2):
                    d = d2 * 2 + e
                    at = (q, slice(d * hidden, (d + 1) * hidden), slice(r2 * cols, (r2 + 1) * cols))
                    oh_s[at] = o_hi[rows, e * cols : (e + 1) * cols]
                    ol_s[at] = o_lo[rows, e * cols : (e + 1) * cols]
    for q in range(4):
        first = dot(wt_s[...], oh_s[q])
        update = first[:channels] + first[channels:] + dot(wt_s[0:channels], ol_s[q])
        update = update.T * (1.0 / seqs)
        mid = pair_ref[q].reshape(2 * cols, channels) + update + ob_ref[...]
        n_hi, n_lo = split(normalize(mid))
        pre = dot(jnp.concatenate([n_hi, n_lo], axis=1), u_s[0 : 2 * channels])
        pre = pre + dot(n_hi, u_s[2 * channels :])
        h_hi, h_lo = split(jnp.maximum(pre + eb_ref[...], 0.0))
        wide = dot(h_hi, d_s[...])
        result = mid + wide[:, :channels] + wide[:, channels:] + dot(h_lo, d_s[:, 0:channels])
        out_ref[q] = result.reshape(2, cols, channels)


def pair_update(left, right, pair_state, w, ob, up, eb, down):
    rows, cols, channels = pair_state.shape
    seqs, groups, lanes = left.shape
    hidden = right.shape[1]
    ft = up.shape[1]
    view = pair_state.reshape(4, rows // 4, cols, channels)
    block = pl.BlockSpec((4, 2, cols, channels), lambda i: (0, i, 0, 0))
    out = pl.pallas_call(
        pair_kernel,
        grid=(rows // 8,),
        in_specs=[
            full(left.shape),
            full(right.shape),
            block,
            full(w.shape),
            full((1, channels)),
            full(up.shape),
            full((1, ft)),
            full(down.shape),
        ],
        out_specs=block,
        out_shape=jax.ShapeDtypeStruct(view.shape, F32),
        scratch_shapes=[
            pltpu.VMEM((groups * lanes, 4 * seqs), BF16),
            pltpu.VMEM((4 * seqs, hidden * cols), BF16),
            pltpu.VMEM((2 * channels, hidden * hidden), BF16),
            pltpu.VMEM((3 * channels, ft), BF16),
            pltpu.VMEM((ft, 2 * channels), BF16),
            pltpu.VMEM((4, hidden * hidden, 2 * cols), BF16),
            pltpu.VMEM((4, hidden * hidden, 2 * cols), BF16),
        ],
        compiler_params=pltpu.CompilerParams(vmem_limit_bytes=VMEM_LIMIT),
        name="pair_update",
    )(left, right, view, w, ob.reshape(1, channels), up, eb.reshape(1, ft), down)
    return out.reshape(pair_state.shape)


def per_device(
    homolog_embedding,
    pair_state,
    probe_projector,
    lookup_projector,
    content_projector,
    sigmoid_projector,
    sigmoid_offset,
    pair_bias_weight,
    mixing_projector,
    mixing_offset,
    first_factor_projector,
    second_factor_projector,
    outer_product_weight,
    outer_product_bias,
    up_weight,
    expand_bias,
    down_weight,
):
    heads = pair_bias_weight.shape[1]
    wide_size = lax.axis_size("wide")
    bias = pair_bias(pair_state, pair_bias_weight.T)
    qkv, gate = project(
        homolog_embedding,
        probe_projector,
        lookup_projector,
        content_projector,
        sigmoid_projector,
        sigmoid_offset,
        heads,
    )
    qkv_all, bias_all = exchange_heads(qkv, bias, wide_size)
    mixed = attention(qkv_all, bias_all)
    back = exchange_back(mixed)
    after, left, right = mix(
        back,
        gate,
        homolog_embedding,
        mixing_projector,
        mixing_offset,
        first_factor_projector,
        second_factor_projector,
    )
    left_all, right_all = exchange_factors(left, right, wide_size)
    left_all = left_all.reshape(-1, *left_all.shape[2:])
    pair_next = pair_update(
        left_all,
        right_all,
        pair_state,
        outer_product_weight,
        outer_product_bias,
        up_weight,
        expand_bias,
        down_weight,
    )
    return after, pair_next


def solution(mesh):
    split_spec = P("wide", "narrow", None)
    return jax.shard_map(
        per_device,
        mesh=mesh,
        in_specs=(split_spec, split_spec) + (P(),) * 15,
        out_specs=(split_spec, split_spec),
        check_vma=False,
    )
```

time: 406 us -> 185 us (0.46); the launches traced: 399 us -> 183 us
  Pallas kernels: 0 us -> 181 us
  matrix products: 180 us -> 0 us
  waiting for transfers between devices: 56.4 us -> 0 us
  local copies, waits for them, and re-layouts: 51.2 us -> 1.51 us
  blocking collectives: 37.2 us -> 0 us
  starting transfers between devices: 26.1 us -> 0 us
  other arithmetic: 25.4 us -> 0 us
  between operations: 14.8 us -> 0.68 us
  loops' own time: 7.86 us -> 0 us
    pallas_call x0 -> x8, Pallas kernels: none -> 181 us  [the longest x1 55.6 us: exchange_heads(): pl.pallas_call(heads_kernel, in_specs=[whole(), whole()], out_specs=[whol...]
    dot_general x34 -> x0, matrix products: 180 us -> none  [the longest x11 96.8 us: matrix_multiply(): jnp.dot(first_arr, second_arr, precision=finest_precision, preferred_elem...]
    all_to_all x6 -> x0, waiting for transfers between devices: 46.7 us -> none  [the longest x1 11 us: copy_for_each(): lax.all_to_all(jnp.broadcast_to(x[None], (devices, *x.shape)), axis, 0, 0...]
    all_to_all x3 -> x0, blocking collectives: 37.2 us -> none  [the longest x1 13.5 us: per_device(): lax.all_to_all(outcome, 'narrow', split_axis=1, concat_axis=2, tiled=True)]
    all_to_all x6 -> x0, starting transfers between devices: 26.1 us -> none  [the longest x1 6.47 us: per_device(): lax.all_to_all(left_rows, 'wide', split_axis=2, concat_axis=0, tiled=True)]
    reduce_sum x15 -> x0, other arithmetic: 19.5 us -> none  [the longest x3 8.11 us: layer_normalize(): row_mean = jnp.mean(tensor, axis=-1, keepdims=True)]
    dynamic_slice x28 -> x0, local copies, waits for them, and re-layouts: 16.6 us -> none  [the longest x8 9.43 us: per_device(): outcome = lax.map(per_item, (operands[0], operands[1], operands[2]))]
    while x10 -> x0, local copies, waits for them, and re-layouts: 14.2 us -> none  [the longest x4 11.1 us: per_device(): outcome = lax.map(per_item, (operands[0], operands[1], operands[2]))]
  transfers between devices with their start and end apart: 7 -> 0, of which waited for: 7 -> 0; matrix products, arithmetic and copies ran while one was open for 5% -> 0% of each run, Pallas kernels for 0% -> 0%
where the time goes in v1:
time: 185 us; the launch traced here: 183 us
  Pallas kernels  181 us (98%)
    pallas_call x1, Pallas kernels, exchange_heads(): pl.pallas_call(heads_kernel, in_specs=[whole(), whole()], out_specs=[whol...  55.6 us
    pallas_call x1, Pallas kernels, pair_update(): pl.pallas_call(pair_kernel, grid=(rows // 8,), in_specs=[full(left.shape)...  53.7 us
    pallas_call x1, Pallas kernels, exchange_factors(): pl.pallas_call(factors_kernel, in_specs=[whole(), whole()], out_specs=[wh...  26.3 us
    pallas_call x1, Pallas kernels, attention(): pl.pallas_call(attention_kernel, grid=(blocks,), in_specs=[full(qkv.shape...  18.4 us
    pallas_call x1, Pallas kernels, exchange_back(): pl.pallas_call(swap_kernel, in_specs=[whole()], out_specs=whole(pl.ANY),...  11.7 us
    pallas_call x1, Pallas kernels, pair_bias(): pl.pallas_call(bias_kernel, grid=(rows // step,), in_specs=[pl.BlockSpec(...  7.71 us
    pallas_call x1, Pallas kernels, project(): pl.pallas_call(project_kernel, in_specs=[whole()] * 6, out_specs=[whole()...  3.87 us

profile of v1, /device:TPU:1, one launch (start us, length us, event | category | flops | bytes accessed | tf_op | source)
XLA Modules:
  0.0 182.9 jit_solution(7598644724968766109)
XLA Ops:
  0.6 3.9 %project.1 = (f32[8,4,96,128]{3,2,1,0:T(8,128)}, f32[4,128,256]{2,1,0:T(8,128)}) custom-call(f32[4,128,256]{2,1,0:T(8,128)} %x_ref.3, f32[256,256]{1,0:T(8,128)} %q_ref.1, f32[256,256]{1,0:T(8,128)} %k_ref.1, f32[256,256]{1,0:T(8,128)} %v_ref.1, f32[256,256]{1,0:T(8,128)} %g_ref.1, f32[1,256]{1,0:T(1,128)} %bitcast.14), custom_call_target="tpu_custom_call" | custom-call | tf_op jit(solution)/shard_map/project/pallas_call | solution.py:116
  4.5 7.7 %pair_bias.1.bias = f32[8,64,128]{2,1,0:T(8,128)} custom-call(f32[64,128,128]{2,1,0:T(8,128)} %pair_ref.1, f32[8,128]{1,0:T(8,128)} %bitcast.11), custom_call_target="tpu_custom_call" | custom-call | tf_op jit(solution)/shard_map/pair_bias/pallas_call | solution.py:74
  12.2 0.0 copy-start
  12.2 55.6 %exchange_heads.1 = (f32[8,4,96,128]{3,2,1,0:T(8,128)}, f32[1024,1024]{1,0:T(8,128)}) custom-call(f32[8,4,96,128]{3,2,1,0:T(8,128)} %get-tuple-element.11.qkv, f32[8,64,128]{2,1,0:T(8,128)} %pair_bias.1.bias), custom_call_target="tpu_custom_call" | custom-call | tf_op jit(solution)/shard_map/exchange_heads/pallas_call | solution.py:290
  67.8 0.0 copy-start.1
  67.8 18.4 %attention.1.src = f32[8,4,32,128]{3,2,1,0:T(8,128)} custom-call(f32[8,4,96,128]{3,2,1,0:T(8,128)} %get-tuple-element.12.qkv_ref, f32[1024,1024]{1,0:T(8,128)} %get-tuple-element.13.bias_ref), custom_call_target="tpu_custom_call" | custom-call | tf_op jit(solution)/shard_map/attention/pallas_call | solution.py:467
  86.2 11.7 %exchange_back.1.o_ref = f32[8,4,32,128]{3,2,1,0:T(8,128)} custom-call(f32[8,4,32,128]{3,2,1,0:T(8,128)} %attention.1.src), custom_call_target="tpu_custom_call" | custom-call | tf_op jit(solution)/shard_map/exchange_back/pallas_call | solution.py:326
  97.9 0.0 copy-done
  97.9 0.8 copy.19.f_ref
  98.7 0.0 copy-done.1
  98.7 0.7 copy.20.s_ref
  99.4 3.5 %mix.1 = (f32[4,128,256]{2,1,0:T(8,128)}, f32[2,4,16,128]{3,2,1,0:T(8,128)}, f32[4,32,128]{2,1,0:T(8,128)}) custom-call(f32[8,4,32,128]{3,2,1,0:T(8,128)} %exchange_back.1.o_ref, f32[4,128,256]{2,1,0:T(8,128)} %get-tuple-element.14.gate_ref, f32[4,128,256]{2,1,0:T(8,128)} %x_ref.3, f32[256,256]{1,0:T(8,128)} %w_ref.2, f32[1,256]{1,0:T(1,128)} %bitcast.13, ...), custom_call_target="tpu_custom_call" | custom-call | tf_op jit(solution)/shard_map/mix/pallas_call | solution.py:518
  102.9 26.3 %exchange_factors.1 = (f32[16,4,16,128]{3,2,1,0:T(8,128)}, f32[64,32,128]{2,1,0:T(8,128)}) custom-call(f32[2,4,16,128]{3,2,1,0:T(8,128)} %get-tuple-element.16.left, f32[4,32,128]{2,1,0:T(8,128)} %get-tuple-element.17.right), custom_call_target="tpu_custom_call" | custom-call | tf_op jit(solution)/shard_map/exchange_factors/pallas_call | solution.py:416
  129.2 53.7 %pair_update.1 = f32[4,16,128,128]{3,2,1,0:T(8,128)} custom-call(f32[64,16,128]{2,1,0:T(8,128)} %bitcast.10, f32[64,32,128]{2,1,0:T(8,128)} %get-tuple-element.19.right_ref, f32[4,16,128,128]{3,2,1,0:T(8,128)} %bitcast.8, f32[1024,128]{1,0:T(8,128)} %w_ref.3, f32[1,128]{1,0:T(1,128)} %bitcast.15, f32[128,512]{1,0:T(8,128)} %up_ref.1, f32[1,512]{1,0:T(1,128)} %bitcast.12, ...), custom_call_target="tpu_custom_call" | custom-call | tf_op jit(solution)/shard_map/pair_update/pallas_call | solution.py:597
Async XLA Ops:
  12.2 85.7 %copy-start = (f32[256,32]{0,1:T(8,128)S(1)}, f32[256,32]{0,1:T(8,128)}, u32[]{:S(2)}) copy-start(f32[256,32]{0,1:T(8,128)} %param.27) | copy-start | bytes 98308
  67.8 30.9 %copy-start.1 = (f32[256,32]{0,1:T(8,128)S(1)}, f32[256,32]{0,1:T(8,128)}, u32[]{:S(2)}) copy-start(f32[256,32]{0,1:T(8,128)} %param.28) | copy-start | bytes 98308

commit v2 on v1

--- a/solution.py
+++ b/solution.py
@@ -11,7 +11,7 @@
 F32 = jnp.float32
 BF16 = jnp.bfloat16
 LOG2E = math.log2(math.e)
-VMEM_LIMIT = 60 * 1024 * 1024
+MIB = 1024 * 1024
 MESH = pl.DeviceIdType.MESH
 
 NT = (((1,), (1,)), ((), ()))
@@ -19,6 +19,10 @@
 
 def dot(a, b):
     return jnp.dot(a, b, preferred_element_type=F32)
+
+
+def dot_nt(a, b):
+    return lax.dot_general(a, b, NT, preferred_element_type=F32)
 
 
 def split(x):
@@ -51,79 +55,16 @@
     return pl.BlockSpec(shape, lambda *_: (0,) * len(shape))
 
 
-def bias_kernel(pair_ref, weight_ref, out_ref):
-    rows, cols, channels = pair_ref.shape
-    heads = weight_ref.shape[0]
-    normed = normalize(pair_ref[...].reshape(rows * cols, channels))
-    n_hi, n_lo = split(normed)
-    stacked = jnp.concatenate([n_hi, n_lo], axis=1)
-    w_hi, w_lo = split32(weight_ref[...] * LOG2E)
+def bias_rows(pair, w_t):
+    rows, cols, channels = pair.shape
+    heads = w_t.shape[0]
+    n_hi, n_lo = split(normalize(pair.reshape(rows * cols, channels)))
+    w_hi, w_lo = split32(w_t * LOG2E)
     top = jnp.concatenate([w_hi, w_hi], axis=1)
     low = jnp.concatenate([w_lo, jnp.zeros_like(w_lo)], axis=1)
     weights = jnp.concatenate([top, low], axis=0).astype(BF16)
-    both = lax.dot_general(weights, stacked, NT, preferred_element_type=F32)
-    result = both[:heads] + both[heads:]
-    for row in range(rows):
-        out_ref[:, row, :] = result[:, row * cols : (row + 1) * cols]
-
-
-def pair_bias(pair_state, weight_t):
-    rows, cols, channels = pair_state.shape
-    heads = weight_t.shape[0]
-    step = 8
-    return pl.pallas_call(
-        bias_kernel,
-        grid=(rows // step,),
-        in_specs=[
-            pl.BlockSpec((step, cols, channels), lambda i: (i, 0, 0)),
-            full((heads, channels)),
-        ],
-        out_specs=pl.BlockSpec((heads, step, cols), lambda i: (0, i, 0)),
-        out_shape=jax.ShapeDtypeStruct((heads, rows, cols), F32),
-        compiler_params=pltpu.CompilerParams(vmem_limit_bytes=VMEM_LIMIT),
-        name="pair_bias",
-    )(pair_state, weight_t)
-
-
-def project_kernel(x_ref, q_ref, k_ref, v_ref, g_ref, off_ref, out_ref, gate_ref):
-    seqs, res, channels = x_ref.shape
-    heads = out_ref.shape[0]
-    width = channels // heads
-    per_tile = 128 // width
-    normed = normalize(x_ref[...].reshape(seqs * res, channels))
-    n_hi, n_lo = split(normed)
-    scale = LOG2E / math.sqrt(width)
-    for kind, ref in enumerate((q_ref, k_ref, v_ref)):
-        w_hi, w_lo = split(ref[...])
-        y = dot3(n_hi, n_lo, w_hi, w_lo)
-        if kind == 0:
-            y = y * scale
-        for s in range(seqs):
-            for tile in range(channels // 128):
-                part = y[s * res : (s + 1) * res, tile * 128 : (tile + 1) * 128].T
-                for h in range(per_tile):
-                    out_ref[tile * per_tile + h, s, kind * width : (kind + 1) * width, :] = part[
-                        h * width : (h + 1) * width
-                    ]
-    w_hi, w_lo = split(g_ref[...])
-    gate = jax.nn.sigmoid(dot3(n_hi, n_lo, w_hi, w_lo) + off_ref[...])
-    gate_ref[...] = gate.reshape(seqs, res, channels)
-
-
-def project(x, wq, wk, wv, wg, offset, heads):
-    seqs, res, channels = x.shape
-    width = channels // heads
-    return pl.pallas_call(
-        project_kernel,
-        in_specs=[whole()] * 6,
-        out_specs=[whole(), whole()],
-        out_shape=[
-            jax.ShapeDtypeStruct((heads, seqs, 3 * width, res), F32),
-            jax.ShapeDtypeStruct((seqs, res, channels), F32),
-        ],
-        compiler_params=pltpu.CompilerParams(vmem_limit_bytes=VMEM_LIMIT),
-        name="project",
-    )(x, wq, wk, wv, wg, offset.reshape(1, channels))
+    both = dot_nt(weights, jnp.concatenate([n_hi, n_lo], axis=1))
+    return both[:heads] + both[heads:]
 
 
 def place(wide, narrow):
@@ -150,7 +91,7 @@
     return z, x, core, at, up, down, far
 
 
-def gather_wide(buf, rows, send, recv):
+def gather_wide(buf, rows, send, recv, source=None, then=None):
     wide, narrow = lax.axis_index("wide"), lax.axis_index("narrow")
     z, x, core, at, up, down, far = wide_links(wide)
     other_x, other_core = 1 - x, 1 - core
@@ -178,10 +119,12 @@
         remote(region, region, send.at[index], recv.at[index], core_dev).wait_recv()
 
     own = slab(z, x, core)
-    push(own, 1, up_dev)
-    push(own, 2, down_dev)
-    push(own, 0, x_dev)
-    push(own, 9, core_dev)
+    for index, dev in ((0, x_dev), (1, up_dev), (2, down_dev), (9, core_dev)):
+        copy = remote(own if source is None else source, own, send.at[index], recv.at[index], dev)
+        copy.start()
+        started.append(copy)
+    if then is not None:
+        then()
     expected = [(slab(z, x, other_core), 9)]
 
     def side(s, x_):
@@ -242,30 +185,80 @@
     return [place(wide, narrow ^ k) for k in range(1, 8)]
 
 
-def heads_kernel(qkv, bias, qkv_out, bias_out, local, b_send, b_recv, q_send, q_recv, send, recv):
+BIAS_STEP = 32
+
+
+def heads_kernel(
+    x, wq, wk, wv, wg, offset, pair, weight, qkv_out, bias_out, gate_out,
+    x_s, w_s, wb_s, tile, qkv, bias,
+    load, load_w, local, b_send, b_recv, q_send, q_recv, send, recv,
+):
     wide, narrow = lax.axis_index("wide"), lax.axis_index("narrow")
     rows, cols = bias.shape[1:]
+    seqs, res, channels = x.shape
+    heads = qkv.shape[0]
+    width = channels // heads
+    per_tile = 128 // width
+    parts = rows // BIAS_STEP
+    first_loads = [pltpu.make_async_copy(x, x_s, load_w.at[4])]
+    for index, w in enumerate((wq, wk, wv, wg)):
+        first_loads.append(pltpu.make_async_copy(w, w_s.at[index], load_w.at[index]))
+    first_loads.append(pltpu.make_async_copy(weight, wb_s, load_w.at[5]))
+    for copy in first_loads:
+        copy.start()
+    loads = []
+    for part in range(parts):
+        span = pl.ds(part * BIAS_STEP, BIAS_STEP)
+        copy = pltpu.make_async_copy(pair.at[span], tile.at[span], load.at[part])
+        copy.start()
+        loads.append(copy)
+    for copy in first_loads:
+        copy.wait()
+
+    n_hi, n_lo = split(normalize(x_s[...].reshape(seqs * res, channels)))
+    scale = LOG2E / math.sqrt(width)
+    for kind in range(3):
+        y = dot3(n_hi, n_lo, *split(w_s[kind]))
+        if kind == 0:
+            y = y * scale
+        for s in range(seqs):
+            for t in range(channels // 128):
+                turned = y[s * res : (s + 1) * res, t * 128 : (t + 1) * 128].T
+                for h in range(per_tile):
+                    qkv[t * per_tile + h, s, kind * width : (kind + 1) * width, :] = turned[
+                        h * width : (h + 1) * width
+                    ]
     greet(narrow_peers() + wide_peers())
+    copies = []
+
+    def send_qkv(ks):
+        for k in ks:
+            peer = narrow ^ k
+            copy = remote(
+                qkv.at[peer], qkv_out.at[narrow], q_send.at[k], q_recv.at[k], place(wide, peer)
+            )
+            copy.start()
+            copies.append(copy)
+
+    send_qkv((1, 2, 6))
+    own_qkv = pltpu.make_async_copy(qkv.at[narrow], qkv_out.at[narrow], local.at[1])
+    own_qkv.start()
+    for part in range(parts):
+        loads[part].wait()
+        first = part * BIAS_STEP
+        result = bias_rows(tile[first : first + BIAS_STEP], wb_s[...])
+        for row in range(BIAS_STEP):
+            bias[:, first + row, :] = result[:, row * cols : (row + 1) * cols]
 
     def bias_slot(source):
         return bias_out.at[pl.ds(wide * rows, rows), pl.ds(source * cols, cols)]
 
     own_bias = pltpu.make_async_copy(bias.at[narrow], bias_slot(narrow), local.at[0])
     own_bias.start()
-    copies = []
-    for k in range(1, 8):
+    for k in (1, 3, 7, 5, 2, 6, 4):
         peer = narrow ^ k
         copy = remote(
             bias.at[peer], bias_slot(narrow), b_send.at[k], b_recv.at[k], place(wide, peer)
-        )
-        copy.start()
-        copies.append(copy)
-    own_qkv = pltpu.make_async_copy(qkv.at[narrow], qkv_out.at[narrow], local.at[1])
-    own_qkv.start()
-    for k in range(1, 8):
-        peer = narrow ^ k
-        copy = remote(
-            qkv.at[peer], qkv_out.at[narrow], q_send.at[k], q_recv.at[k], place(wide, peer)
         )
         copy.start()
         copies.append(copy)
@@ -273,7 +266,13 @@
     for k in range(1, 8):
         slot = bias_slot(narrow ^ k)
         remote(slot, slot, b_send.at[k], b_recv.at[k], place(wide, narrow ^ k)).wait_recv()
-    gather_wide(bias_out, rows, send, recv)
+
+    def rest():
+        send_qkv((3, 7, 5, 4))
+        gate = dot3(n_hi, n_lo, *split(w_s[3])) + offset[...]
+        gate_out[...] = jax.nn.sigmoid(gate).reshape(seqs, res, channels)
+
+    gather_wide(bias_out, rows, send, recv, then=rest)
     for k in range(1, 8):
         slot = qkv_out.at[narrow ^ k]
         remote(slot, slot, q_send.at[k], q_recv.at[k], place(wide, narrow ^ k)).wait_recv()
@@ -285,22 +284,43 @@
 DMA = pltpu.SemaphoreType.DMA
 
 
-def exchange_heads(qkv, bias, wide_size):
-    heads, rows, cols = bias.shape
+def exchange_heads(x, wq, wk, wv, wg, offset, pair_state, weight_t, wide_size):
+    rows, cols, _ = pair_state.shape
+    heads, pair_channels = weight_t.shape
+    seqs, res, channels = x.shape
+    width = channels // heads
+    qkv = (heads, seqs, 3 * width, res)
     return pl.pallas_call(
         heads_kernel,
-        in_specs=[whole(), whole()],
-        out_specs=[whole(pl.ANY), whole(pl.ANY)],
+        in_specs=[whole(pltpu.HBM)] * 5 + [whole(), whole(pltpu.HBM), whole(pltpu.HBM)],
+        out_specs=[whole(pl.ANY), whole(pl.ANY), whole()],
         out_shape=[
-            jax.ShapeDtypeStruct(qkv.shape, F32),
+            jax.ShapeDtypeStruct(qkv, F32),
             jax.ShapeDtypeStruct((wide_size * rows, heads * cols), F32),
+            jax.ShapeDtypeStruct(x.shape, F32),
         ],
-        scratch_shapes=[DMA((2,)), DMA((8,)), DMA((8,)), DMA((8,)), DMA((8,)), DMA((19,)), DMA((19,))],
+        scratch_shapes=[
+            pltpu.VMEM(x.shape, F32),
+            pltpu.VMEM((4, channels, channels), F32),
+            pltpu.VMEM((heads, pair_channels), F32),
+            pltpu.VMEM(pair_state.shape, F32),
+            pltpu.VMEM(qkv, F32),
+            pltpu.VMEM((heads, rows, cols), F32),
+            DMA((rows // BIAS_STEP,)),
+            DMA((6,)),
+            DMA((2,)),
+            DMA((8,)),
+            DMA((8,)),
+            DMA((8,)),
+            DMA((8,)),
+            DMA((19,)),
+            DMA((19,)),
+        ],
         compiler_params=pltpu.CompilerParams(
-            collective_id=0, has_side_effects=True, vmem_limit_bytes=VMEM_LIMIT
+            collective_id=0, has_side_effects=True, vmem_limit_bytes=54 * MIB
         ),
         name="exchange_heads",
-    )(qkv, bias)
+    )(x, wq, wk, wv, wg, offset.reshape(1, channels), pair_state, weight_t)
 
 
 def swap_kernel(src, out, local, send, recv):
@@ -330,7 +350,7 @@
         out_shape=jax.ShapeDtypeStruct(src.shape, F32),
         scratch_shapes=[DMA, DMA((8,)), DMA((8,))],
         compiler_params=pltpu.CompilerParams(
-            collective_id=1, has_side_effects=True, vmem_limit_bytes=VMEM_LIMIT
+            collective_id=1, has_side_effects=True, vmem_limit_bytes=6 * MIB
         ),
         name="exchange_back",
     )(src)
@@ -368,23 +388,25 @@
         )
 
     own_left = pltpu.make_async_copy(left.at[wide % 2], left_out.at[wide], local.at[1])
-    for k in range(8):
-        for half in range(2):
-            me = jnp.logical_and(selfish, wide % 2 == half) if k == 0 else None
-            if me is None:
-                left_copy(half, k).start()
-            else:
-
-                @pl.when(jnp.logical_not(me))
-                def _():
+
+    def send_left():
+        for k in (5, 4, 7, 6, 3, 2, 1, 0):
+            for half in range(2):
+                if k:
                     left_copy(half, k).start()
-
-                @pl.when(me)
-                def _():
-                    own_left.start()
-
+                else:
+                    me = jnp.logical_and(selfish, wide % 2 == half)
+
+                    @pl.when(jnp.logical_not(me))
+                    def _():
+                        left_copy(half, k).start()
+
+                    @pl.when(me)
+                    def _():
+                        own_left.start()
+
+    gather_wide(right_out, seqs, send, recv, source=right, then=send_left)
     own_right.wait()
-    gather_wide(right_out, seqs, send, recv)
 
     for w in range(16):
         me = jnp.logical_and(selfish, wide == w)
@@ -423,7 +445,7 @@
         ],
         scratch_shapes=[DMA((2,)), DMA((2, 8)), DMA((16,)), DMA((19,)), DMA((19,))],
         compiler_params=pltpu.CompilerParams(
-            collective_id=2, has_side_effects=True, vmem_limit_bytes=VMEM_LIMIT
+            collective_id=2, has_side_effects=True, vmem_limit_bytes=8 * MIB
         ),
         name="exchange_factors",
     )(left, right)
@@ -448,16 +470,20 @@
                 v_s[s, cols, :] = jnp.concatenate([v_hi, v_lo, one, pad], axis=0).T.astype(BF16)
                 w_s[s, cols, :] = jnp.concatenate([v_hi, pad, one, pad], axis=0).T.astype(BF16)
 
-    block = pl.program_id(0)
-    bias = bias_ref[...]
-    start = pl.multiple_of(block * res, res)
+    step = pl.program_id(0)
+    rows = bias_ref.shape[0]
+    start = pl.multiple_of(step * rows, rows)
+    def sequence(s):
+        scores = dot(q_s[s, pl.ds(start, rows), :], k_s[s]) + bias_ref[...]
+        top = jnp.max(scores, axis=-1, keepdims=True)
+        p_hi, p_lo = split(jnp.exp2(scores - top))
+        mixed = (dot(p_hi, v_s[s]) + dot(p_lo, w_s[s])).T
+        mixed = (mixed[:width] + mixed[width : 2 * width]) / mixed[2 * width : 3 * width]
+        for b in range(rows // res):
+            out_ref[b, s] = mixed[:, b * res : (b + 1) * res]
+
     for s in range(seqs):
-        scores = dot(q_s[s, pl.ds(start, res), :], k_s[s]) + bias
-        top = jnp.max(scores, axis=-1, keepdims=True)
-        weights = jnp.exp2(scores - top)
-        p_hi, p_lo = split(weights)
-        mixed = (dot(p_hi, v_s[s]) + dot(p_lo, w_s[s])).T
-        out_ref[0, s] = (mixed[:width] + mixed[width : 2 * width]) / mixed[2 * width : 3 * width]
+        pl.when(step >= 0)(functools.partial(sequence, s))
 
 
 def attention(qkv, bias):
@@ -466,9 +492,9 @@
     span = blocks * res
     return pl.pallas_call(
         attention_kernel,
-        grid=(blocks,),
-        in_specs=[full(qkv.shape), pl.BlockSpec((res, span), lambda i: (i, 0))],
-        out_specs=pl.BlockSpec((1, seqs, width, res), lambda i: (i, 0, 0, 0)),
+        grid=(blocks // 4,),
+        in_specs=[full(qkv.shape), pl.BlockSpec((4 * res, span), lambda i: (i, 0))],
+        out_specs=pl.BlockSpec((4, seqs, width, res), lambda i: (i, 0, 0, 0)),
         out_shape=jax.ShapeDtypeStruct((blocks, seqs, width, res), F32),
         scratch_shapes=[
             pltpu.VMEM((seqs, span, 4 * width), BF16),
@@ -476,7 +502,7 @@
             pltpu.VMEM((seqs, span, 4 * width), BF16),
             pltpu.VMEM((seqs, span, 4 * width), BF16),
         ],
-        compiler_params=pltpu.CompilerParams(vmem_limit_bytes=VMEM_LIMIT),
+        compiler_params=pltpu.CompilerParams(vmem_limit_bytes=44 * MIB),
         name="attention",
     )(qkv, bias)
 
@@ -496,10 +522,9 @@
     next_ref[...] = after.reshape(seqs, res, channels)
     n_hi, n_lo = split(normalize(after))
     first = f_ref[...]
-    factors = jnp.concatenate([first] * 4 + [s_ref[...]] * 4, axis=1)
-    f_hi, f_lo = split(factors)
-    y = dot3(n_hi, n_lo, f_hi, f_lo)
-    hidden = first.shape[1]
+    f_hi, f_lo = split(jnp.concatenate([first] * 4 + [s_ref[...]] * 4, axis=0))
+    y = dot_nt(n_hi, f_hi) + dot_nt(n_hi, f_lo) + dot_nt(n_lo, f_hi)
+    hidden = first.shape[0]
     quarter = lax.broadcasted_iota(jnp.int32, (res // 8, 128), 1) // hidden
     for s in range(seqs):
         left = y[s * res : (s + 1) * res, :128]
@@ -524,35 +549,49 @@
             jax.ShapeDtypeStruct((2, seqs, res // 8, 128), F32),
             jax.ShapeDtypeStruct((seqs, hidden, res), F32),
         ],
-        compiler_params=pltpu.CompilerParams(vmem_limit_bytes=VMEM_LIMIT),
+        compiler_params=pltpu.CompilerParams(vmem_limit_bytes=16 * MIB),
         name="mix",
-    )(o, gate, x, w, offset.reshape(1, channels), first, second)
+    )(o, gate, x, w, offset.reshape(1, channels), first.T, second.T)
 
 
 def pair_kernel(
     left_ref, right_ref, pair_ref, w_ref, ob_ref, up_ref, eb_ref, down_ref, out_ref,
-    l_s, r_s, wt_s, u_s, d_s, oh_s, ol_s,
+    l_s, r_s, wt_s, u_s, d_s, oh_s, ol_s, mid_s,
 ):
-    seqs, groups, _ = left_ref.shape
-    hidden, cols = right_ref.shape[1:]
-    channels = pair_ref.shape[-1]
+    cols, channels = pair_ref.shape[2:]
+    seqs = r_s.shape[0] // 4
+    groups = left_ref.shape[0] // seqs
+    hidden = right_ref.shape[0] // seqs
     span = hidden * hidden
 
     @pl.when(pl.program_id(0) == 0)
     def _():
-        for r in range(groups):
-            hi, lo = split32(left_ref[:, r, :])
-            l_s[r * 128 : (r + 1) * 128, 0:128] = jnp.concatenate([hi, hi], axis=0).T.astype(BF16)
-            l_s[r * 128 : (r + 1) * 128, 128:256] = jnp.concatenate([lo, lo], axis=0).T.astype(BF16)
-        for d in range(hidden):
-            hi, lo = split(right_ref[:, d, :])
-            part = slice(d * cols, (d + 1) * cols)
-            r_s[:, part] = jnp.concatenate([hi, lo, hi, lo], axis=0)
-        for b in range(span // 128):
+        def left_rows(r, carry):
+            hi, lo = split32(left_ref[pl.ds(r, seqs, stride=groups), :])
+            at = pl.ds(pl.multiple_of(r * 128, 128), 128)
+            l_s[at, 0:128] = jnp.concatenate([hi, hi], axis=0).T.astype(BF16)
+            l_s[at, 128:256] = jnp.concatenate([lo, lo], axis=0).T.astype(BF16)
+            return carry
+
+        lax.fori_loop(0, groups, left_rows, 0, unroll=4)
+
+        def right_columns(d, carry):
+            hi, lo = split(right_ref[pl.ds(d, seqs, stride=hidden), :])
+            at = pl.ds(pl.multiple_of(d * cols, cols), cols)
+            r_s[:, at] = jnp.concatenate([hi, lo, hi, lo], axis=0)
+            return carry
+
+        lax.fori_loop(0, hidden, right_columns, 0, unroll=4)
+
+        def outer_weights(b, carry):
             rows = [w_ref[pl.ds(b * 4 + e, hidden, stride=hidden), :] for e in range(4)]
             w_hi, w_lo = split32(jnp.concatenate(rows, axis=0).T)
-            wt_s[0:channels, b * 128 : (b + 1) * 128] = w_hi.astype(BF16)
-            wt_s[channels : 2 * channels, b * 128 : (b + 1) * 128] = w_lo.astype(BF16)
+            at = pl.ds(pl.multiple_of(b * 128, 128), 128)
+            wt_s[0:channels, at] = w_hi.astype(BF16)
+            wt_s[channels : 2 * channels, at] = w_lo.astype(BF16)
+            return carry
+
+        lax.fori_loop(0, span // 128, outer_weights, 0, unroll=2)
         u_hi, u_lo = split(up_ref[...])
         u_s[0:channels] = u_hi
         u_s[channels : 2 * channels] = u_hi
@@ -577,20 +616,34 @@
         first = dot(wt_s[...], oh_s[q])
         update = first[:channels] + first[channels:] + dot(wt_s[0:channels], ol_s[q])
         update = update.T * (1.0 / seqs)
-        mid = pair_ref[q].reshape(2 * cols, channels) + update + ob_ref[...]
+        mid_s[q * 2 * cols : (q + 1) * 2 * cols, :] = (
+            pair_ref[q].reshape(2 * cols, channels) + update + ob_ref[...]
+        )
+
+    def transition(part, carry):
+        at = pl.ds(pl.multiple_of(part * 1024, 1024), 1024)
+        mid = mid_s[at, :]
         n_hi, n_lo = split(normalize(mid))
         pre = dot(jnp.concatenate([n_hi, n_lo], axis=1), u_s[0 : 2 * channels])
         pre = pre + dot(n_hi, u_s[2 * channels :])
         h_hi, h_lo = split(jnp.maximum(pre + eb_ref[...], 0.0))
         wide = dot(h_hi, d_s[...])
         result = mid + wide[:, :channels] + wide[:, channels:] + dot(h_lo, d_s[:, 0:channels])
-        out_ref[q] = result.reshape(2, cols, channels)
+        mid_s[at, :] = result
+        return carry
+
+    pl.when(step >= 0)(lambda: transition(0, None) and None)
+
+    for q in range(4):
+        out_ref[q] = mid_s[q * 2 * cols : (q + 1) * 2 * cols, :].reshape(2, cols, channels)
 
 
 def pair_update(left, right, pair_state, w, ob, up, eb, down):
     rows, cols, channels = pair_state.shape
     seqs, groups, lanes = left.shape
     hidden = right.shape[1]
+    left = left.reshape(seqs * groups, lanes)
+    right = right.reshape(seqs * hidden, cols)
     ft = up.shape[1]
     view = pair_state.reshape(4, rows // 4, cols, channels)
     block = pl.BlockSpec((4, 2, cols, channels), lambda i: (0, i, 0, 0))
@@ -617,8 +670,9 @@
             pltpu.VMEM((ft, 2 * channels), BF16),
             pltpu.VMEM((4, hidden * hidden, 2 * cols), BF16),
             pltpu.VMEM((4, hidden * hidden, 2 * cols), BF16),
+            pltpu.VMEM((8 * cols, channels), F32),
         ],
-        compiler_params=pltpu.CompilerParams(vmem_limit_bytes=VMEM_LIMIT),
+        compiler_params=pltpu.CompilerParams(vmem_limit_bytes=48 * MIB),
         name="pair_update",
     )(left, right, view, w, ob.reshape(1, channels), up, eb.reshape(1, ft), down)
     return out.reshape(pair_state.shape)
@@ -643,19 +697,18 @@
     expand_bias,
     down_weight,
 ):
-    heads = pair_bias_weight.shape[1]
     wide_size = lax.axis_size("wide")
-    bias = pair_bias(pair_state, pair_bias_weight.T)
-    qkv, gate = project(
+    qkv_all, bias_all, gate = exchange_heads(
         homolog_embedding,
         probe_projector,
         lookup_projector,
         content_projector,
         sigmoid_projector,
         sigmoid_offset,
-        heads,
+        pair_state,
+        pair_bias_weight.T,
+        wide_size,
     )
-    qkv_all, bias_all = exchange_heads(qkv, bias, wide_size)
     mixed = attention(qkv_all, bias_all)
     back = exchange_back(mixed)
     after, left, right = mix(

time: 185 us -> 130 us (0.70)
  Pallas kernels: 181 us -> 125 us
  local copies, waits for them, and re-layouts: 1.51 us -> 3.64 us
    pallas_call x4 -> x2, Pallas kernels: 85.6 us -> 58.2 us  [the longest x1 48.1 us: exchange_heads(): pl.pallas_call(heads_kernel, in_specs=[whole(pltpu.HBM)] * 5 + [whole(),...]
    pallas_call x1, Pallas kernels: 53.7 us -> 33.1 us  [pair_update(): pl.pallas_call(pair_kernel, grid=(rows // 8,), in_specs=[full(left.shape)...]
    pallas_call x1, Pallas kernels: 26.3 us -> 21.4 us  [exchange_factors(): pl.pallas_call(factors_kernel, in_specs=[whole(), whole()], out_specs=[wh...]
    unnamed x6 -> x26, local copies, waits for them, and re-layouts: 1.51 us -> 3.64 us
    pallas_call x1, Pallas kernels: 3.46 us -> 1.39 us  [mix(): pl.pallas_call(mix_kernel, in_specs=[whole()] * 7, out_specs=[whole()] *...]
where the time goes in v2:
time: 130 us; the launch traced here: 129 us
  Pallas kernels  125 us (96%)
  local copies, waits for them, and re-layouts  3.64 us (3%)
    pallas_call x1, Pallas kernels, exchange_heads(): pl.pallas_call(heads_kernel, in_specs=[whole(pltpu.HBM)] * 5 + [whole(),...  48.1 us
    pallas_call x1, Pallas kernels, pair_update(): pl.pallas_call(pair_kernel, grid=(rows // 8,), in_specs=[full(left.shape)...  33.1 us
    pallas_call x1, Pallas kernels, exchange_factors(): pl.pallas_call(factors_kernel, in_specs=[whole(), whole()], out_specs=[wh...  21.4 us
    pallas_call x1, Pallas kernels, exchange_back(): pl.pallas_call(swap_kernel, in_specs=[whole()], out_specs=whole(pl.ANY),...  10.6 us
    pallas_call x1, Pallas kernels, attention(): pl.pallas_call(attention_kernel, grid=(blocks // 4,), in_specs=[full(qkv....  10.1 us
    unnamed x26, local copies, waits for them, and re-layouts  3.64 us

profile of v2, /device:TPU:1, one launch (start us, length us, event | category | flops | bytes accessed | tf_op | source)
XLA Modules:
  0.0 129.2 jit_solution(15869904176782031159)
XLA Ops:
  0.6 0.0 copy-start.1
  0.6 0.0 copy-start.5
  0.7 0.0 copy-start.8
  0.7 0.0 copy-start.9
  0.7 48.1 %exchange_heads.1 = (f32[8,4,96,128]{3,2,1,0:T(8,128)}, f32[1024,1024]{1,0:T(8,128)}, f32[4,128,256]{2,1,0:T(8,128)}) custom-call(f32[4,128,256]{2,1,0:T(8,128)} %x_ref.1, f32[256,256]{1,0:T(8,128)} %wq.1, f32[256,256]{1,0:T(8,128)} %wk.1, f32[256,256]{1,0:T(8,128)} %wv.1, f32[256,256]{1,0:T(8,128)} %wg.1, f32[1,256]{1,0:T(1,128)} %bitcast.21, ...), custom_call_target="tpu_custom_call" | custom-call | tf_op jit(solution)/shard_map/exchange_heads/pallas_call | solution.py:293
  48.8 0.0 copy-start.11
  48.8 0.0 copy-start
  48.8 2.2 %copy-done = f32[1024,1024]{1,0:T(8,128)S(1)} copy-done((f32[1024,1024]{1,0:T(8,128)S(1)}, f32[1024,1024]{1,0:T(8,128)}, u32[]{:S(2)}) %copy-start) | copy-done | bytes 4194328
  51.0 0.0 copy-start.2
  51.0 1.4 %copy-done.2 = f32[8,4,96,128]{3,2,1,0:T(8,128)S(1)} copy-done((f32[8,4,96,128]{3,2,1,0:T(8,128)S(1)}, f32[8,4,96,128]{3,2,1,0:T(8,128)}, u32[]{:S(2)}) %copy-start.2) | copy-done | bytes 1572888
  52.4 0.0 copy-start.4
  52.4 0.0 copy-start.3
  52.4 0.0 copy-start.6
  52.4 0.0 copy-start.7
  52.4 0.0 copy-start.10
  52.5 0.0 copy-start.12
  52.5 10.1 %attention.1.src = f32[8,4,32,128]{3,2,1,0:T(8,128)S(1)} custom-call(f32[8,4,96,128]{3,2,1,0:T(8,128)S(1)} %copy-done.2, f32[1024,1024]{1,0:T(8,128)S(1)} %copy-done), custom_call_target="tpu_custom_call" | custom-call | tf_op jit(solution)/shard_map/attention/pallas_call | solution.py:493
  62.6 10.6 %exchange_back.1.o_ref = f32[8,4,32,128]{3,2,1,0:T(8,128)S(1)} custom-call(f32[8,4,32,128]{3,2,1,0:T(8,128)S(1)} %attention.1.src), custom_call_target="tpu_custom_call" | custom-call | tf_op jit(solution)/shard_map/exchange_back/pallas_call | solution.py:346
  73.2 0.0 copy-done.1
  73.2 0.0 copy-done.5
  73.2 0.0 copy-done.8
  73.2 0.0 copy-done.9
  73.2 0.0 copy-done.11
  73.2 0.0 copy-done.4
  73.2 1.4 %mix.1 = (f32[4,128,256]{2,1,0:T(8,128)}, f32[2,4,16,128]{3,2,1,0:T(8,128)S(1)}, f32[4,32,128]{2,1,0:T(8,128)S(1)}) custom-call(f32[8,4,32,128]{3,2,1,0:T(8,128)S(1)} %exchange_back.1.o_ref, f32[4,128,256]{2,1,0:T(8,128)S(1)} %copy-done.4, f32[4,128,256]{2,1,0:T(8,128)S(1)} %copy-done.1, f32[256,256]{1,0:T(8,128)S(1)} %copy-done.5, f32[1,256]{1,0:T(1,128)S(1)} %bitcast.16, ...), custom_call_target="tpu_custom_call" | custom-call | tf_op jit(solution)/shard_map/mix/pallas_call | solution.py:543
  74.6 21.4 %exchange_factors.1 = (f32[16,4,16,128]{3,2,1,0:T(8,128)S(1)}, f32[64,32,128]{2,1,0:T(8,128)S(1)}) custom-call(f32[2,4,16,128]{3,2,1,0:T(8,128)S(1)} %get-tuple-element.14.left, f32[4,32,128]{2,1,0:T(8,128)S(1)} %get-tuple-element.15.right), custom_call_target="tpu_custom_call" | custom-call | tf_op jit(solution)/shard_map/exchange_factors/pallas_call | solution.py:438
  96.0 0.0 copy-done.3
  96.1 0.0 copy-done.6
  96.1 0.0 copy-done.7
  96.1 0.0 copy-done.10
  96.1 0.0 copy-done.12
  96.1 33.1 %pair_update.1 = f32[4,16,128,128]{3,2,1,0:T(8,128)} custom-call(f32[1024,128]{1,0:T(8,128)S(1)} %bitcast.12, f32[2048,128]{1,0:T(8,128)S(1)} %bitcast.11, f32[4,16,128,128]{3,2,1,0:T(8,128)} %bitcast.18, f32[1024,128]{1,0:T(8,128)S(1)} %copy-done.3, f32[1,128]{1,0:T(1,128)S(1)} %bitcast.17, f32[128,512]{1,0:T(8,128)S(1)} %copy-done.6, ...), custom_call_target="tpu_custom_call" | custom-call | tf_op jit(solution)/shard_map/pair_update/pallas_call | solution.py:650
Async XLA Ops:
  0.6 72.5 %copy-start.1 = (f32[4,128,256]{2,1,0:T(8,128)S(1)}, f32[4,128,256]{2,1,0:T(8,128)}, u32[]{:S(2)}) copy-start(f32[4,128,256]{2,1,0:T(8,128)} %x_ref.1) | copy-start | bytes 1572868
  0.6 72.5 %copy-start.5 = (f32[256,256]{1,0:T(8,128)S(1)}, f32[256,256]{1,0:T(8,128)}, u32[]{:S(2)}) copy-start(f32[256,256]{1,0:T(8,128)} %w_ref.2) | copy-start | bytes 786436
  0.7 72.5 %copy-start.8 = (f32[256,32]{0,1:T(8,128)S(1)}, f32[256,32]{0,1:T(8,128)}, u32[]{:S(2)}) copy-start(f32[256,32]{0,1:T(8,128)} %param.27) | copy-start | bytes 98308
  0.7 72.5 %copy-start.9 = (f32[256,32]{0,1:T(8,128)S(1)}, f32[256,32]{0,1:T(8,128)}, u32[]{:S(2)}) copy-start(f32[256,32]{0,1:T(8,128)} %param.28) | copy-start | bytes 98308
  48.8 24.4 %copy-start.11 = (f32[256]{0:T(256)S(1)}, f32[256]{0:T(256)}, u32[]{:S(2)}) copy-start(f32[256]{0:T(256)} %param.26) | copy-start | bytes 3076
  48.8 2.2 %copy-start = (f32[1024,1024]{1,0:T(8,128)S(1)}, f32[1024,1024]{1,0:T(8,128)}, u32[]{:S(2)}) copy-start(f32[1024,1024]{1,0:T(8,128)} %get-tuple-element.11.bias_ref) | copy-start | bytes 12582916
  51.0 1.4 %copy-start.2 = (f32[8,4,96,128]{3,2,1,0:T(8,128)S(1)}, f32[8,4,96,128]{3,2,1,0:T(8,128)}, u32[]{:S(2)}) copy-start(f32[8,4,96,128]{3,2,1,0:T(8,128)} %get-tuple-element.10.qkv_ref) | copy-start | bytes 4718596
  52.4 20.8 %copy-start.4 = (f32[4,128,256]{2,1,0:T(8,128)S(1)}, f32[4,128,256]{2,1,0:T(8,128)}, u32[]{:S(2)}) copy-start(f32[4,128,256]{2,1,0:T(8,128)} %get-tuple-element.12.gate_ref) | copy-start | bytes 1572868
  52.4 43.6 %copy-start.3 = (f32[1024,128]{1,0:T(8,128)S(1)}, f32[1024,128]{1,0:T(8,128)}, u32[]{:S(2)}) copy-start(f32[1024,128]{1,0:T(8,128)} %w_ref.3) | copy-start | bytes 1572868
  52.4 43.6 %copy-start.6 = (f32[128,512]{1,0:T(8,128)S(1)}, f32[128,512]{1,0:T(8,128)}, u32[]{:S(2)}) copy-start(f32[128,512]{1,0:T(8,128)} %up_ref.1) | copy-start | bytes 786436
  52.4 43.6 %copy-start.7 = (f32[512,128]{1,0:T(8,128)S(1)}, f32[512,128]{1,0:T(8,128)}, u32[]{:S(2)}) copy-start(f32[512,128]{1,0:T(8,128)} %down_ref.1) | copy-start | bytes 786436
  52.4 43.6 %copy-start.10 = (f32[512]{0:T(512)S(1)}, f32[512]{0:T(512)}, u32[]{:S(2)}) copy-start(f32[512]{0:T(512)} %param.32) | copy-start | bytes 6148
  52.5 43.6 %copy-start.12 = (f32[128]{0:T(128)S(1)}, f32[128]{0:T(128)}, u32[]{:S(2)}) copy-start(f32[128]{0:T(128)} %param.30) | copy-start | bytes 1540

commit v3 on v2

--- a/solution.py
+++ b/solution.py
@@ -323,40 +323,10 @@
     )(x, wq, wk, wv, wg, offset.reshape(1, channels), pair_state, weight_t)
 
 
-def swap_kernel(src, out, local, send, recv):
-    wide, narrow = lax.axis_index("wide"), lax.axis_index("narrow")
-    greet(narrow_peers())
-    copies = []
-    for k in range(1, 8):
-        peer = narrow ^ k
-        copy = remote(src.at[peer], out.at[narrow], send.at[k], recv.at[k], place(wide, peer))
-        copy.start()
-        copies.append(copy)
-    own = pltpu.make_async_copy(src.at[narrow], out.at[narrow], local)
-    own.start()
-    for k in range(1, 8):
-        slot = out.at[narrow ^ k]
-        remote(slot, slot, send.at[k], recv.at[k], place(wide, narrow ^ k)).wait_recv()
-    own.wait()
-    for copy in copies:
-        copy.wait_send()
-
-
-def exchange_back(src):
-    return pl.pallas_call(
-        swap_kernel,
-        in_specs=[whole()],
-        out_specs=whole(pl.ANY),
-        out_shape=jax.ShapeDtypeStruct(src.shape, F32),
-        scratch_shapes=[DMA, DMA((8,)), DMA((8,))],
-        compiler_params=pltpu.CompilerParams(
-            collective_id=1, has_side_effects=True, vmem_limit_bytes=6 * MIB
-        ),
-        name="exchange_back",
-    )(src)
-
-
-def factors_kernel(left, right, left_out, right_out, local, l_send, l_recv, send, recv):
+def factors_kernel(
+    left, right, outer_w, up, down, left_out, right_out, wt_out, u_out, d_out,
+    local, l_send, l_recv, send, recv,
+):
     wide, narrow = lax.axis_index("wide"), lax.axis_index("narrow")
     seqs = right.shape[0]
     barrier = pltpu.get_barrier_semaphore()
@@ -405,7 +375,24 @@
                     def _():
                         own_left.start()
 
-    gather_wide(right_out, seqs, send, recv, source=right, then=send_left)
+    def weights():
+        send_left()
+        span, channels = outer_w.shape
+        hidden = right.shape[1]
+        for b in range(span // 128):
+            rows = [outer_w[pl.ds(b * 4 + e, hidden, stride=hidden), :] for e in range(4)]
+            w_hi, w_lo = split32(jnp.concatenate(rows, axis=0).T)
+            wt_out[0:channels, b * 128 : (b + 1) * 128] = w_hi.astype(BF16)
+            wt_out[channels : 2 * channels, b * 128 : (b + 1) * 128] = w_lo.astype(BF16)
+        u_hi, u_lo = split(up[...])
+        u_out[0:channels] = u_hi
+        u_out[channels : 2 * channels] = u_hi
+        u_out[2 * channels :] = u_lo
+        d_hi, d_lo = split(down[...])
+        d_out[:, 0:channels] = d_hi
+        d_out[:, channels:] = d_lo
+
+    gather_wide(right_out, seqs, send, recv, source=right, then=weights)
     own_right.wait()
 
     for w in range(16):
@@ -434,56 +421,94 @@
                     left_copy(half, k).wait_send()
 
 
-def exchange_factors(left, right, wide_size):
+def exchange_factors(left, right, w, up, down, wide_size):
+    span, channels = w.shape
+    ft = up.shape[1]
     return pl.pallas_call(
         factors_kernel,
-        in_specs=[whole(), whole()],
-        out_specs=[whole(pl.ANY), whole(pl.ANY)],
+        in_specs=[whole()] * 5,
+        out_specs=[whole(pl.ANY)] * 2 + [whole()] * 3,
         out_shape=[
             jax.ShapeDtypeStruct((wide_size, *left.shape[1:]), F32),
             jax.ShapeDtypeStruct((wide_size * right.shape[0], *right.shape[1:]), F32),
+            jax.ShapeDtypeStruct((2 * channels, span), BF16),
+            jax.ShapeDtypeStruct((3 * channels, ft), BF16),
+            jax.ShapeDtypeStruct((ft, 2 * channels), BF16),
         ],
         scratch_shapes=[DMA((2,)), DMA((2, 8)), DMA((16,)), DMA((19,)), DMA((19,))],
         compiler_params=pltpu.CompilerParams(
-            collective_id=2, has_side_effects=True, vmem_limit_bytes=8 * MIB
+            collective_id=2, has_side_effects=True, vmem_limit_bytes=16 * MIB
         ),
         name="exchange_factors",
-    )(left, right)
-
-
-def attention_kernel(qkv_ref, bias_ref, out_ref, q_s, k_s, v_s, w_s):
+    )(left, right, w, up, down)
+
+
+ATTENTION_ROWS = 512
+
+
+def attention_kernel(qkv_ref, bias_ref, back, q_s, k_s, v_s, w_s, o_s, local, send, recv):
+    wide, narrow = lax.axis_index("wide"), lax.axis_index("narrow")
     blocks, seqs, stacked, res = qkv_ref.shape
     width = stacked // 3
-
-    @pl.when(pl.program_id(0) == 0)
-    def _():
-        pad = jnp.zeros((width, res), F32)
+    pad = jnp.zeros((width, res), F32)
+    one = jnp.ones_like(pad)
+    for s in range(seqs):
+        for b in range(blocks):
+            cols = slice(b * res, (b + 1) * res)
+            q_hi, q_lo = split32(qkv_ref[b, s, 0:width, :])
+            k_hi, k_lo = split32(qkv_ref[b, s, width : 2 * width, :])
+            v_hi, v_lo = split32(qkv_ref[b, s, 2 * width :, :])
+            q_s[s, cols, :] = jnp.concatenate([q_hi, q_hi, q_lo, q_lo], axis=0).T.astype(BF16)
+            k_s[s, :, cols] = jnp.concatenate([k_hi, k_lo, k_hi, k_lo], axis=0).astype(BF16)
+            v_s[s, cols, :] = jnp.concatenate([v_hi, v_lo, one, pad], axis=0).T.astype(BF16)
+            w_s[s, cols, :] = jnp.concatenate([v_hi, pad, one, pad], axis=0).T.astype(BF16)
+    greet(narrow_peers())
+    rows = ATTENTION_ROWS
+    group = rows // res
+
+    def piece(n, s):
+        return remote(
+            o_s.at[n, s], back.at[narrow, s], send.at[n, s], recv.at[narrow, s], place(wide, n)
+        )
+
+    def each(step, act):
+        for b in range(group):
+            n = step * group + b
+            pl.when(n != narrow)(functools.partial(act, n))
+
+    def rows_of(step, carry):
+        start = pl.multiple_of(step * rows, rows)
+
+        def sequence(s):
+            scores = dot(q_s[s, pl.ds(start, rows), :], k_s[s]) + bias_ref[pl.ds(start, rows), :]
+            top = jnp.max(scores, axis=-1, keepdims=True)
+            p_hi, p_lo = split(jnp.exp2(scores - top))
+            mixed = (dot(p_hi, v_s[s]) + dot(p_lo, w_s[s])).T
+            mixed = (mixed[:width] + mixed[width : 2 * width]) / mixed[2 * width : 3 * width]
+            for b in range(group):
+                o_s[step * group + b, s] = mixed[:, b * res : (b + 1) * res]
+
         for s in range(seqs):
-            for b in range(blocks):
-                cols = slice(b * res, (b + 1) * res)
-                q_hi, q_lo = split32(qkv_ref[b, s, 0:width, :])
-                k_hi, k_lo = split32(qkv_ref[b, s, width : 2 * width, :])
-                v_hi, v_lo = split32(qkv_ref[b, s, 2 * width :, :])
-                q_s[s, cols, :] = jnp.concatenate([q_hi, q_hi, q_lo, q_lo], axis=0).T.astype(BF16)
-                k_s[s, :, cols] = jnp.concatenate([k_hi, k_lo, k_hi, k_lo], axis=0).astype(BF16)
-                one = jnp.ones_like(pad)
-                v_s[s, cols, :] = jnp.concatenate([v_hi, v_lo, one, pad], axis=0).T.astype(BF16)
-                w_s[s, cols, :] = jnp.concatenate([v_hi, pad, one, pad], axis=0).T.astype(BF16)
-
-    step = pl.program_id(0)
-    rows = bias_ref.shape[0]
-    start = pl.multiple_of(step * rows, rows)
-    def sequence(s):
-        scores = dot(q_s[s, pl.ds(start, rows), :], k_s[s]) + bias_ref[...]
-        top = jnp.max(scores, axis=-1, keepdims=True)
-        p_hi, p_lo = split(jnp.exp2(scores - top))
-        mixed = (dot(p_hi, v_s[s]) + dot(p_lo, w_s[s])).T
-        mixed = (mixed[:width] + mixed[width : 2 * width]) / mixed[2 * width : 3 * width]
-        for b in range(rows // res):
-            out_ref[b, s] = mixed[:, b * res : (b + 1) * res]
-
-    for s in range(seqs):
-        pl.when(step >= 0)(functools.partial(sequence, s))
+            pl.when(step >= 0)(functools.partial(sequence, s))
+            if s:
+                each(step, lambda n, s=s: piece(n, s - 1).start())
+        each(step, lambda n: piece(n, 0).wait_send())
+        each(step, lambda n: piece(n, seqs - 1).start())
+        return carry
+
+    lax.fori_loop(0, blocks // group, rows_of, 0)
+    own = pltpu.make_async_copy(o_s.at[narrow], back.at[narrow], local)
+    own.start()
+    for k in range(1, 8):
+        peer = narrow ^ k
+        for s in range(1, seqs):
+            piece(peer, s).wait_send()
+    for k in range(1, 8):
+        peer = narrow ^ k
+        for s in range(seqs):
+            slot = back.at[peer, s]
+            remote(slot, slot, send.at[peer, s], recv.at[peer, s], place(wide, peer)).wait_recv()
+    own.wait()
 
 
 def attention(qkv, bias):
@@ -492,17 +517,22 @@
     span = blocks * res
     return pl.pallas_call(
         attention_kernel,
-        grid=(blocks // 4,),
-        in_specs=[full(qkv.shape), pl.BlockSpec((4 * res, span), lambda i: (i, 0))],
-        out_specs=pl.BlockSpec((4, seqs, width, res), lambda i: (i, 0, 0, 0)),
+        in_specs=[whole(), whole()],
+        out_specs=whole(pl.ANY),
         out_shape=jax.ShapeDtypeStruct((blocks, seqs, width, res), F32),
         scratch_shapes=[
             pltpu.VMEM((seqs, span, 4 * width), BF16),
             pltpu.VMEM((seqs, 4 * width, span), BF16),
             pltpu.VMEM((seqs, span, 4 * width), BF16),
             pltpu.VMEM((seqs, span, 4 * width), BF16),
+            pltpu.VMEM((blocks, seqs, width, res), F32),
+            DMA,
+            DMA((blocks, seqs)),
+            DMA((blocks, seqs)),
         ],
-        compiler_params=pltpu.CompilerParams(vmem_limit_bytes=44 * MIB),
+        compiler_params=pltpu.CompilerParams(
+            collective_id=1, has_side_effects=True, vmem_limit_bytes=56 * MIB
+        ),
         name="attention",
     )(qkv, bias)
 
@@ -555,14 +585,13 @@
 
 
 def pair_kernel(
-    left_ref, right_ref, pair_ref, w_ref, ob_ref, up_ref, eb_ref, down_ref, out_ref,
-    l_s, r_s, wt_s, u_s, d_s, oh_s, ol_s, mid_s,
+    left_ref, right_ref, pair_ref, wt_s, ob_ref, u_s, eb_ref, d_s, out_ref,
+    l_s, r_s, oh_s, ol_s, mid_s,
 ):
     cols, channels = pair_ref.shape[2:]
     seqs = r_s.shape[0] // 4
     groups = left_ref.shape[0] // seqs
     hidden = right_ref.shape[0] // seqs
-    span = hidden * hidden
 
     @pl.when(pl.program_id(0) == 0)
     def _():
@@ -582,23 +611,6 @@
             return carry
 
         lax.fori_loop(0, hidden, right_columns, 0, unroll=4)
-
-        def outer_weights(b, carry):
-            rows = [w_ref[pl.ds(b * 4 + e, hidden, stride=hidden), :] for e in range(4)]
-            w_hi, w_lo = split32(jnp.concatenate(rows, axis=0).T)
-            at = pl.ds(pl.multiple_of(b * 128, 128), 128)
-            wt_s[0:channels, at] = w_hi.astype(BF16)
-            wt_s[channels : 2 * channels, at] = w_lo.astype(BF16)
-            return carry
-
-        lax.fori_loop(0, span // 128, outer_weights, 0, unroll=2)
-        u_hi, u_lo = split(up_ref[...])
-        u_s[0:channels] = u_hi
-        u_s[channels : 2 * channels] = u_hi
-        u_s[2 * channels :] = u_lo
-        d_hi, d_lo = split(down_ref[...])
-        d_s[:, 0:channels] = d_hi
-        d_s[:, channels:] = d_lo
 
     step = pl.program_id(0)
     lhs = l_s[pl.ds(pl.multiple_of(step * 256, 256), 256), :]
@@ -638,7 +650,7 @@
         out_ref[q] = mid_s[q * 2 * cols : (q + 1) * 2 * cols, :].reshape(2, cols, channels)
 
 
-def pair_update(left, right, pair_state, w, ob, up, eb, down):
+def pair_update(left, right, pair_state, wt, ob, up, eb, down):
     rows, cols, channels = pair_state.shape
     seqs, groups, lanes = left.shape
     hidden = right.shape[1]
@@ -654,7 +666,7 @@
             full(left.shape),
             full(right.shape),
             block,
-            full(w.shape),
+            full(wt.shape),
             full((1, channels)),
             full(up.shape),
             full((1, ft)),
@@ -665,16 +677,13 @@
         scratch_shapes=[
             pltpu.VMEM((groups * lanes, 4 * seqs), BF16),
             pltpu.VMEM((4 * seqs, hidden * cols), BF16),
-            pltpu.VMEM((2 * channels, hidden * hidden), BF16),
-            pltpu.VMEM((3 * channels, ft), BF16),
-            pltpu.VMEM((ft, 2 * channels), BF16),
             pltpu.VMEM((4, hidden * hidden, 2 * cols), BF16),
             pltpu.VMEM((4, hidden * hidden, 2 * cols), BF16),
             pltpu.VMEM((8 * cols, channels), F32),
         ],
         compiler_params=pltpu.CompilerParams(vmem_limit_bytes=48 * MIB),
         name="pair_update",
-    )(left, right, view, w, ob.reshape(1, channels), up, eb.reshape(1, ft), down)
+    )(left, right, view, wt, ob.reshape(1, channels), up, eb.reshape(1, ft), down)
     return out.reshape(pair_state.shape)
 
 
@@ -709,8 +718,7 @@
         pair_bias_weight.T,
         wide_size,
     )
-    mixed = attention(qkv_all, bias_all)
-    back = exchange_back(mixed)
+    back = attention(qkv_all, bias_all)
     after, left, right = mix(
         back,
         gate,
@@ -720,17 +728,19 @@
         first_factor_projector,
         second_factor_projector,
     )
-    left_all, right_all = exchange_factors(left, right, wide_size)
+    left_all, right_all, wt, up, down = exchange_factors(
+        left, right, outer_product_weight, up_weight, down_weight, wide_size
+    )
     left_all = left_all.reshape(-1, *left_all.shape[2:])
     pair_next = pair_update(
         left_all,
         right_all,
         pair_state,
-        outer_product_weight,
+        wt,
         outer_product_bias,
-        up_weight,
+        up,
         expand_bias,
-        down_weight,
+        down,
     )
     return after, pair_next
 

time: 130 us -> 127 us (0.977)
  local copies, waits for them, and re-layouts: 3.64 us -> 1.1 us
    unnamed x26 -> x24, local copies, waits for them, and re-layouts: 3.64 us -> 1.1 us
    pallas_call x3 -> x2, Pallas kernels: 42.1 us -> 43.1 us  [the longest x1 25.6 us: exchange_factors(): pl.pallas_call(factors_kernel, in_specs=[whole()] * 5, out_specs=[whole(p...]
where the time goes in v3:
time: 127 us
  Pallas kernels  125 us (98%)
    pallas_call x1, Pallas kernels, exchange_heads(): pl.pallas_call(heads_kernel, in_specs=[whole(pltpu.HBM)] * 5 + [whole(),...  48.1 us
    pallas_call x1, Pallas kernels, pair_update(): pl.pallas_call(pair_kernel, grid=(rows // 8,), in_specs=[full(left.shape)...  32.4 us
    pallas_call x1, Pallas kernels, exchange_factors(): pl.pallas_call(factors_kernel, in_specs=[whole()] * 5, out_specs=[whole(p...  25.6 us
    pallas_call x1, Pallas kernels, attention(): pl.pallas_call(attention_kernel, in_specs=[whole(), whole()], out_specs=w...  17.5 us

profile of v3, /device:TPU:1, one launch (start us, length us, event | category | flops | bytes accessed | tf_op | source)
XLA Modules:
  0.0 126.9 jit_solution(3534438854200588788)
XLA Ops:
  0.6 48.1 %exchange_heads.1 = (f32[8,4,96,128]{3,2,1,0:T(8,128)}, f32[1024,1024]{1,0:T(8,128)}, f32[4,128,256]{2,1,0:T(8,128)}) custom-call(f32[4,128,256]{2,1,0:T(8,128)} %x_ref.1, f32[256,256]{1,0:T(8,128)} %wq.1, f32[256,256]{1,0:T(8,128)} %wk.1, f32[256,256]{1,0:T(8,128)} %wv.1, f32[256,256]{1,0:T(8,128)} %wg.1, f32[1,256]{1,0:T(1,128)} %bitcast.21, ...), custom_call_target="tpu_custom_call" | custom-call | tf_op jit(solution)/shard_map/exchange_heads/pallas_call | solution.py:293
  48.7 0.0 copy-start.1
  48.7 0.0 copy-start.2
  48.8 0.0 copy-start.4
  48.8 0.0 copy-start.7
  48.8 0.0 copy-start.8
  48.8 0.0 copy-start.10
  48.8 0.0 copy-start.3
  48.8 0.0 copy-start.5
  48.8 0.0 copy-start.6
  48.8 0.0 copy-start.9
  48.9 0.0 copy-start.11
  48.9 17.5 %attention.1.o_ref = f32[8,4,32,128]{3,2,1,0:T(8,128)} custom-call(f32[8,4,96,128]{3,2,1,0:T(8,128)} %get-tuple-element.13.qkv_ref, f32[1024,1024]{1,0:T(8,128)} %get-tuple-element.14.bias_ref), custom_call_target="tpu_custom_call" | custom-call | tf_op jit(solution)/shard_map/attention/pallas_call | solution.py:518
  66.4 0.0 copy-done.1
  66.4 0.0 copy-done.2
  66.4 0.0 copy-done.4
  66.4 0.0 copy-done.7
  66.4 0.0 copy-done.8
  66.4 0.0 copy-done.10
  66.4 0.0 copy-start
  66.4 1.0 copy-done
  67.5 1.4 %mix.1 = (f32[4,128,256]{2,1,0:T(8,128)}, f32[2,4,16,128]{3,2,1,0:T(8,128)S(1)}, f32[4,32,128]{2,1,0:T(8,128)S(1)}) custom-call(f32[8,4,32,128]{3,2,1,0:T(8,128)S(1)} %copy-done, f32[4,128,256]{2,1,0:T(8,128)S(1)} %copy-done.2, f32[4,128,256]{2,1,0:T(8,128)S(1)} %copy-done.1, f32[256,256]{1,0:T(8,128)S(1)} %copy-done.4, f32[1,256]{1,0:T(1,128)S(1)} %bitcast.16, ...), custom_call_target="tpu_custom_call" | custom-call | tf_op jit(solution)/shard_map/mix/pallas_call | solution.py:573
  68.9 0.0 copy-done.3
  68.9 0.0 copy-done.5
  68.9 0.0 copy-done.6
  68.9 25.6 %exchange_factors.1 = (f32[16,4,16,128]{3,2,1,0:T(8,128)S(1)}, f32[64,32,128]{2,1,0:T(8,128)S(1)}, bf16[256,1024]{1,0:T(8,128)(2,1)S(1)}, bf16[384,512]{1,0:T(8,128)(2,1)S(1)}, bf16[512,256]{1,0:T(8,128)(2,1)S(1)}) custom-call(f32[2,4,16,128]{3,2,1,0:T(8,128)S(1)} %get-tuple-element.17.left, f32[4,32,128]{2,1,0:T(8,128)S(1)} %get-tuple-element.18.right, ...), custom_call_target="tpu_custom_call" | custom-call | tf_op jit(solution)/shard_map/exchange_factors/pallas_call | solution.py:427
  94.4 0.0 copy-done.9
  94.5 0.0 copy-done.11
  94.5 32.4 %pair_update.1 = f32[4,16,128,128]{3,2,1,0:T(8,128)} custom-call(f32[1024,128]{1,0:T(8,128)S(1)} %bitcast.12, f32[2048,128]{1,0:T(8,128)S(1)} %bitcast.11, f32[4,16,128,128]{3,2,1,0:T(8,128)} %bitcast.18, bf16[256,1024]{1,0:T(8,128)(2,1)S(1)} %get-tuple-element.21.wt_s, f32[1,128]{1,0:T(1,128)S(1)} %bitcast.17, bf16[384,512]{1,0:T(8,128)(2,1)S(1)} %get-tuple-element.22.u_s, ...), custom_call_target="tpu_custom_call" | custom-call | tf_op jit(solution)/shard_map/pair_update/pallas_call | solution.py:662
Async XLA Ops:
  48.7 17.6 %copy-start.1 = (f32[4,128,256]{2,1,0:T(8,128)S(1)}, f32[4,128,256]{2,1,0:T(8,128)}, u32[]{:S(2)}) copy-start(f32[4,128,256]{2,1,0:T(8,128)} %x_ref.1) | copy-start | bytes 1572868
  48.7 17.6 %copy-start.2 = (f32[4,128,256]{2,1,0:T(8,128)S(1)}, f32[4,128,256]{2,1,0:T(8,128)}, u32[]{:S(2)}) copy-start(f32[4,128,256]{2,1,0:T(8,128)} %get-tuple-element.15.gate_ref) | copy-start | bytes 1572868
  48.8 17.6 %copy-start.4 = (f32[256,256]{1,0:T(8,128)S(1)}, f32[256,256]{1,0:T(8,128)}, u32[]{:S(2)}) copy-start(f32[256,256]{1,0:T(8,128)} %w_ref.1) | copy-start | bytes 786436
  48.8 17.6 %copy-start.7 = (f32[256,32]{0,1:T(8,128)S(1)}, f32[256,32]{0,1:T(8,128)}, u32[]{:S(2)}) copy-start(f32[256,32]{0,1:T(8,128)} %param.27) | copy-start | bytes 98308
  48.8 17.6 %copy-start.8 = (f32[256,32]{0,1:T(8,128)S(1)}, f32[256,32]{0,1:T(8,128)}, u32[]{:S(2)}) copy-start(f32[256,32]{0,1:T(8,128)} %param.28) | copy-start | bytes 98308
  48.8 17.6 %copy-start.10 = (f32[256]{0:T(256)S(1)}, f32[256]{0:T(256)}, u32[]{:S(2)}) copy-start(f32[256]{0:T(256)} %param.26) | copy-start | bytes 3076
  48.8 20.1 %copy-start.3 = (f32[1024,128]{1,0:T(8,128)S(1)}, f32[1024,128]{1,0:T(8,128)}, u32[]{:S(2)}) copy-start(f32[1024,128]{1,0:T(8,128)} %outer_w.1) | copy-start | bytes 1572868
  48.8 20.1 %copy-start.5 = (f32[128,512]{1,0:T(8,128)S(1)}, f32[128,512]{1,0:T(8,128)}, u32[]{:S(2)}) copy-start(f32[128,512]{1,0:T(8,128)} %up.1) | copy-start | bytes 786436
  48.8 20.0 %copy-start.6 = (f32[512,128]{1,0:T(8,128)S(1)}, f32[512,128]{1,0:T(8,128)}, u32[]{:S(2)}) copy-start(f32[512,128]{1,0:T(8,128)} %down.1) | copy-start | bytes 786436
  48.8 45.6 %copy-start.9 = (f32[512]{0:T(512)S(1)}, f32[512]{0:T(512)}, u32[]{:S(2)}) copy-start(f32[512]{0:T(512)} %param.32) | copy-start | bytes 6148
  48.9 45.6 %copy-start.11 = (f32[128]{0:T(128)S(1)}, f32[128]{0:T(128)}, u32[]{:S(2)}) copy-start(f32[128]{0:T(128)} %param.30) | copy-start | bytes 1540
  66.4 1.0 copy-start

commit v4 on v3

--- a/solution.py
+++ b/solution.py
@@ -71,11 +71,14 @@
     return {"wide": wide, "narrow": narrow}
 
 
-def greet(peers):
+def announce(peers):
     barrier = pltpu.get_barrier_semaphore()
     for peer in peers:
         pl.semaphore_signal(barrier, inc=1, device_id=peer, device_id_type=MESH)
-    pl.semaphore_wait(barrier, len(peers))
+
+
+def await_peers(peers):
+    pl.semaphore_wait(pltpu.get_barrier_semaphore(), len(peers))
 
 
 def remote(src, dst, send, recv, peer):
@@ -200,6 +203,8 @@
     width = channels // heads
     per_tile = 128 // width
     parts = rows // BIAS_STEP
+    peers = narrow_peers() + wide_peers()
+    announce(peers)
     first_loads = [pltpu.make_async_copy(x, x_s, load_w.at[4])]
     for index, w in enumerate((wq, wk, wv, wg)):
         first_loads.append(pltpu.make_async_copy(w, w_s.at[index], load_w.at[index]))
@@ -228,7 +233,7 @@
                     qkv[t * per_tile + h, s, kind * width : (kind + 1) * width, :] = turned[
                         h * width : (h + 1) * width
                     ]
-    greet(narrow_peers() + wide_peers())
+    await_peers(peers)
     copies = []
 
     def send_qkv(ks):
@@ -450,6 +455,8 @@
     wide, narrow = lax.axis_index("wide"), lax.axis_index("narrow")
     blocks, seqs, stacked, res = qkv_ref.shape
     width = stacked // 3
+    peers = narrow_peers()
+    announce(peers)
     pad = jnp.zeros((width, res), F32)
     one = jnp.ones_like(pad)
     for s in range(seqs):
@@ -462,7 +469,7 @@
             k_s[s, :, cols] = jnp.concatenate([k_hi, k_lo, k_hi, k_lo], axis=0).astype(BF16)
             v_s[s, cols, :] = jnp.concatenate([v_hi, v_lo, one, pad], axis=0).T.astype(BF16)
             w_s[s, cols, :] = jnp.concatenate([v_hi, pad, one, pad], axis=0).T.astype(BF16)
-    greet(narrow_peers())
+    await_peers(peers)
     rows = ATTENTION_ROWS
     group = rows // res
 

time: 127 us -> 124 us (0.976)
  Pallas kernels: 125 us -> 121 us
    pallas_call x1, Pallas kernels: 48.1 us -> 45.4 us  [exchange_heads(): pl.pallas_call(heads_kernel, in_specs=[whole(pltpu.HBM)] * 5 + [whole(),...]
    pallas_call x1, Pallas kernels: 25.6 us -> 23.5 us  [exchange_factors(): pl.pallas_call(factors_kernel, in_specs=[whole()] * 5, out_specs=[whole(p...]
    pallas_call x1, Pallas kernels: 17.5 us -> 18.8 us  [attention(): pl.pallas_call(attention_kernel, in_specs=[whole(), whole()], out_specs=w...]
where the time goes in v4:
time: 124 us; the launch traced here: 123 us
  Pallas kernels  121 us (98%)
    pallas_call x1, Pallas kernels, exchange_heads(): pl.pallas_call(heads_kernel, in_specs=[whole(pltpu.HBM)] * 5 + [whole(),...  45.4 us
    pallas_call x1, Pallas kernels, pair_update(): pl.pallas_call(pair_kernel, grid=(rows // 8,), in_specs=[full(left.shape)...  32.4 us
    pallas_call x1, Pallas kernels, exchange_factors(): pl.pallas_call(factors_kernel, in_specs=[whole()] * 5, out_specs=[whole(p...  23.5 us
    pallas_call x1, Pallas kernels, attention(): pl.pallas_call(attention_kernel, in_specs=[whole(), whole()], out_specs=w...  18.8 us

profile of v4, /device:TPU:1, one launch (start us, length us, event | category | flops | bytes accessed | tf_op | source)
XLA Modules:
  0.0 123.4 jit_solution(11494649522197130655)
XLA Ops:
  0.6 45.4 %exchange_heads.1 = (f32[8,4,96,128]{3,2,1,0:T(8,128)}, f32[1024,1024]{1,0:T(8,128)}, f32[4,128,256]{2,1,0:T(8,128)}) custom-call(f32[4,128,256]{2,1,0:T(8,128)} %x_ref.1, f32[256,256]{1,0:T(8,128)} %wq.1, f32[256,256]{1,0:T(8,128)} %wk.1, f32[256,256]{1,0:T(8,128)} %wv.1, f32[256,256]{1,0:T(8,128)} %wg.1, f32[1,256]{1,0:T(1,128)} %bitcast.21, ...), custom_call_target="tpu_custom_call" | custom-call | tf_op jit(solution)/shard_map/exchange_heads/pallas_call | solution.py:298
  46.0 0.0 copy-start.1
  46.0 0.0 copy-start.2
  46.0 0.0 copy-start.4
  46.0 0.0 copy-start.7
  46.0 0.0 copy-start.8
  46.0 0.0 copy-start.10
  46.1 0.0 copy-start.3
  46.1 0.0 copy-start.5
  46.1 0.0 copy-start.6
  46.1 0.0 copy-start.9
  46.1 0.0 copy-start.11
  46.1 18.8 %attention.1.o_ref = f32[8,4,32,128]{3,2,1,0:T(8,128)} custom-call(f32[8,4,96,128]{3,2,1,0:T(8,128)} %get-tuple-element.13.qkv_ref, f32[1024,1024]{1,0:T(8,128)} %get-tuple-element.14.bias_ref), custom_call_target="tpu_custom_call" | custom-call | tf_op jit(solution)/shard_map/attention/pallas_call | solution.py:525
  64.9 0.0 copy-done.1
  64.9 0.0 copy-done.2
  65.0 0.0 copy-done.4
  65.0 0.0 copy-done.7
  65.0 0.0 copy-done.8
  65.0 0.0 copy-done.10
  65.0 0.0 copy-start
  65.0 1.0 copy-done
  66.0 1.4 %mix.1 = (f32[4,128,256]{2,1,0:T(8,128)}, f32[2,4,16,128]{3,2,1,0:T(8,128)S(1)}, f32[4,32,128]{2,1,0:T(8,128)S(1)}) custom-call(f32[8,4,32,128]{3,2,1,0:T(8,128)S(1)} %copy-done, f32[4,128,256]{2,1,0:T(8,128)S(1)} %copy-done.2, f32[4,128,256]{2,1,0:T(8,128)S(1)} %copy-done.1, f32[256,256]{1,0:T(8,128)S(1)} %copy-done.4, f32[1,256]{1,0:T(1,128)S(1)} %bitcast.16, ...), custom_call_target="tpu_custom_call" | custom-call | tf_op jit(solution)/shard_map/mix/pallas_call | solution.py:580
  67.4 0.0 copy-done.3
  67.4 0.0 copy-done.5
  67.4 0.0 copy-done.6
  67.4 23.5 %exchange_factors.1 = (f32[16,4,16,128]{3,2,1,0:T(8,128)S(1)}, f32[64,32,128]{2,1,0:T(8,128)S(1)}, bf16[256,1024]{1,0:T(8,128)(2,1)S(1)}, bf16[384,512]{1,0:T(8,128)(2,1)S(1)}, bf16[512,256]{1,0:T(8,128)(2,1)S(1)}) custom-call(f32[2,4,16,128]{3,2,1,0:T(8,128)S(1)} %get-tuple-element.17.left, f32[4,32,128]{2,1,0:T(8,128)S(1)} %get-tuple-element.18.right, ...), custom_call_target="tpu_custom_call" | custom-call | tf_op jit(solution)/shard_map/exchange_factors/pallas_call | solution.py:432
  91.0 0.0 copy-done.9
  91.0 0.0 copy-done.11
  91.0 32.4 %pair_update.1 = f32[4,16,128,128]{3,2,1,0:T(8,128)} custom-call(f32[1024,128]{1,0:T(8,128)S(1)} %bitcast.12, f32[2048,128]{1,0:T(8,128)S(1)} %bitcast.11, f32[4,16,128,128]{3,2,1,0:T(8,128)} %bitcast.18, bf16[256,1024]{1,0:T(8,128)(2,1)S(1)} %get-tuple-element.21.wt_s, f32[1,128]{1,0:T(1,128)S(1)} %bitcast.17, bf16[384,512]{1,0:T(8,128)(2,1)S(1)} %get-tuple-element.22.u_s, ...), custom_call_target="tpu_custom_call" | custom-call | tf_op jit(solution)/shard_map/pair_update/pallas_call | solution.py:669
Async XLA Ops:
  46.0 18.9 %copy-start.1 = (f32[4,128,256]{2,1,0:T(8,128)S(1)}, f32[4,128,256]{2,1,0:T(8,128)}, u32[]{:S(2)}) copy-start(f32[4,128,256]{2,1,0:T(8,128)} %x_ref.1) | copy-start | bytes 1572868
  46.0 18.9 %copy-start.2 = (f32[4,128,256]{2,1,0:T(8,128)S(1)}, f32[4,128,256]{2,1,0:T(8,128)}, u32[]{:S(2)}) copy-start(f32[4,128,256]{2,1,0:T(8,128)} %get-tuple-element.15.gate_ref) | copy-start | bytes 1572868
  46.0 18.9 %copy-start.4 = (f32[256,256]{1,0:T(8,128)S(1)}, f32[256,256]{1,0:T(8,128)}, u32[]{:S(2)}) copy-start(f32[256,256]{1,0:T(8,128)} %w_ref.1) | copy-start | bytes 786436
  46.0 18.9 %copy-start.7 = (f32[256,32]{0,1:T(8,128)S(1)}, f32[256,32]{0,1:T(8,128)}, u32[]{:S(2)}) copy-start(f32[256,32]{0,1:T(8,128)} %param.27) | copy-start | bytes 98308
  46.0 18.9 %copy-start.8 = (f32[256,32]{0,1:T(8,128)S(1)}, f32[256,32]{0,1:T(8,128)}, u32[]{:S(2)}) copy-start(f32[256,32]{0,1:T(8,128)} %param.28) | copy-start | bytes 98308
  46.0 18.9 %copy-start.10 = (f32[256]{0:T(256)S(1)}, f32[256]{0:T(256)}, u32[]{:S(2)}) copy-start(f32[256]{0:T(256)} %param.26) | copy-start | bytes 3076
  46.1 21.4 %copy-start.3 = (f32[1024,128]{1,0:T(8,128)S(1)}, f32[1024,128]{1,0:T(8,128)}, u32[]{:S(2)}) copy-start(f32[1024,128]{1,0:T(8,128)} %outer_w.1) | copy-start | bytes 1572868
  46.1 21.4 %copy-start.5 = (f32[128,512]{1,0:T(8,128)S(1)}, f32[128,512]{1,0:T(8,128)}, u32[]{:S(2)}) copy-start(f32[128,512]{1,0:T(8,128)} %up.1) | copy-start | bytes 786436
  46.1 21.4 %copy-start.6 = (f32[512,128]{1,0:T(8,128)S(1)}, f32[512,128]{1,0:T(8,128)}, u32[]{:S(2)}) copy-start(f32[512,128]{1,0:T(8,128)} %down.1) | copy-start | bytes 786436
  46.1 44.9 %copy-start.9 = (f32[512]{0:T(512)S(1)}, f32[512]{0:T(512)}, u32[]{:S(2)}) copy-start(f32[512]{0:T(512)} %param.32) | copy-start | bytes 6148
  46.1 44.9 %copy-start.11 = (f32[128]{0:T(128)S(1)}, f32[128]{0:T(128)}, u32[]{:S(2)}) copy-start(f32[128]{0:T(128)} %param.30) | copy-start | bytes 1540
  65.0 1.0 copy-start
